TPU v7x, 128 devices: a whole 4x4x4 slice. The times are simulated.
128 devices in a mesh: row: 16 (over y, x_lo, core), col: 8 (over x_hi, z).
Axes of the slice: x: 4 (x_hi: 2, x_lo: 2; x = x_hi * 2 + x_lo), y: 4, z: 4, core: 2. Of those that a mesh axis runs over, the one named last changes fastest.
Arguments:
- coeffs: bfloat16 [65536, 2048], P('row', 'col'), may hold values from -0.8984375 to 0.8984375
- occupations: float32 [2048], replicated, may hold values from 0.05 to 2
- block_order: int32 [128], replicated, may hold values from 0 to 127, as said below
- neighbours: int32 [128, 15], P(('row', 'col')), may hold values from 0 to 127, as said below
- counts: int32 [128], P(('row', 'col')), may hold values from 4 to 15, as said below
Outputs:
- density: bfloat16 [128, 15, 512, 512], P(('row', 'col'))
Inputs may be any that keep to these rules, and one draw needn't show every extreme that they name: Within each aligned group of 8 entries, block_order is a permutation of that group's own indices. For atom row block a, the first counts[a] entries of neighbours[a] are distinct blocks b with |b - a| < 8; the remaining entries equal a. `counts`: some block has 15 live slots in every draw.
All inputs are finite; a program needn't handle non-finite values.
Results may differ from a plain program's by a relative error of at most 0.0044.
Values may be sent and summed in bfloat16 or wider, within the bound.
No kernel may reach another device: no remote copies, remote signals or barrier semaphores. Data moves between devices by JAX's collectives and lax.ppermute only.
A program may use at most 128 MiB of HBM per device.

v0:
```python
import functools

import jax
import jax.numpy as jnp
from jax import lax
from jax.experimental import pallas as pl
from jax.experimental.pallas import tpu as pltpu
from jax.sharding import PartitionSpec as P


NNB = 15
BS = 512
COLS = 8
KS = 256
STATES = COLS * KS
AXES = ("row", "col")
TILE = 256


def devices():
    for k in range(8):
        for core in range(2):
            for xh in range(2):
                for z in range(4):
                    yield k, core, xh, z


def index(k, core, xh, z):
    return ((k * 2 + core) * 2 + xh) * 4 + z


def up_of(core):
    return -1 if core else 1


def move_route(dx, up):
    return [
        (index(k, c, x ^ dx, (z - up * up_of(c)) % 4), index(k, c, x, z)) for k, c, x, z in devices()
    ]


def swap_route():
    return [(index(k, c, x, z), index(k, 1 - c, x, z)) for k, c, x, z in devices()]


def partner_of(k, core):
    return (k + 1, 0) if core else (k - 1, 1)


def edge_route():
    pairs = []
    for k, c, x, z in devices():
        to, tc = partner_of(k, c)
        if 0 <= to < 8:
            pairs.append((index(k, c, x, z), index(to, tc, x, z)))
    return pairs


def result_route(t, r):
    pairs = []
    for k, c, x, z in devices():
        j = x * 4 + z
        v = (x ^ t) * 4 + (z + r * up_of(c)) % 4
        if (v > j) != bool(c):
            to, tc = k, 1 - c
        else:
            to, tc = partner_of(k, c)
        if 0 <= to < 8:
            pairs.append((index(k, c, x, z), index(to, tc, x, z)))
    return pairs


def send(value, route):
    return lax.ppermute(value, AXES, route)


def where_am_i():
    core = lax.rem(lax.axis_index("row"), 2)
    j = lax.axis_index("col")
    return core, j, lax.div(j, 4), lax.rem(j, 4)


def around(z, core, ups):
    return lax.rem(z + 4 + jnp.where(core == 0, ups, -ups), 4)


def place(t, r):
    core, j, x, z = where_am_i()
    return core, j, (1 - x if t else x) * 4 + around(z, core, r)


def slot_for(neighbours, counts, offset):
    own = lax.axis_index("row") * COLS + lax.axis_index("col")
    slot = jnp.int32(NNB)
    for s in range(NNB):
        hit = (neighbours[0, s] == own + offset) & (s < counts[0])
        slot = jnp.where(hit, s, slot)
    return slot


def result_slot(neighbours, counts, t, r, opposite):
    _, j, v = place(t, -r if opposite else r)
    return slot_for(neighbours, counts, jnp.where(v < j, 8 + v - j, v - j - 8))


def columns(c):
    return pl.ds(c * KS, KS)


def load(parts, target, sem):
    return [
        pltpu.make_async_copy(ref.at[i], target.at[:, columns(c)], sem)
        for c, (ref, i) in enumerate(parts)
    ]


MIRROR = (0, 3, 2, 1, 4, 7, 6, 5)


def load_mirrored(whole, target, sem):
    return [
        pltpu.make_async_copy(whole.at[:, columns(m)], target.at[:, columns(c)], sem)
        for c, m in enumerate(MIRROR)
    ]


def multiply(left, right, result):
    def step(n, _):
        rows = pl.ds(pl.multiple_of(n * TILE, TILE), TILE)
        result[:, rows] = lax.dot_general(
            left[...], right[rows, :], (((1,), (1,)), ((), ())), preferred_element_type=jnp.float32
        ).astype(jnp.bfloat16)
        return 0

    lax.fori_loop(0, BS // TILE, step, 0)


def pick_kernel(block_order, coeffs, a0, y0, a1, y1, sem):
    core, _, x, z = where_am_i()
    base = lax.axis_index("row") * COLS
    copies = []
    for t, (a, y) in enumerate(((a0, y0), (a1, y1))):
        for ref, rs in ((a, (2, 1)), (y, (3, 0))):
            for i, r in enumerate(rs):
                v = (1 - x if t else x) * 4 + around(z, core, r)
                copies.append(pltpu.make_async_copy(coeffs.at[block_order[base + v] - base], ref.at[i], sem))
    for copy in copies:
        copy.start()
    for copy in copies:
        copy.wait()


def n_arrays(where):
    return max(i for parts in where for i, _ in parts) + 1


def weigh_kernel(where, occupations, *rest):
    refs, (out, block, sem) = rest[:-3], rest[-3:]
    copies = load([(refs[n], i) for n, i in where[0]], block, sem)
    for copy in copies:
        copy.start()
    for copy in copies:
        copy.wait()
    core, _, x, z = where_am_i()
    for c in range(COLS):
        ups = (0, -1, -2, 1)[c % 4]
        source = (1 - x if c // 4 else x) * 4 + around(z, core, ups)
        scale = occupations[pl.ds(source, 1), :]
        out[:, columns(c)] = (block[:, columns(c)].astype(jnp.float32) * scale).astype(jnp.bfloat16)


def own_kernel(blocks, first, where, neighbours, counts, weights, *rest):
    n = len(blocks)
    refs, rest = rest[: n_arrays(where)], rest[n_arrays(where) :]
    if not first:
        rest = rest[1:]
    out, left, right, result, left_sem, sem, out_sem = rest
    slots = []
    for b, (t, r) in enumerate(blocks):
        _, j, v = place(t, r)
        slots.append(slot_for(neighbours, counts, v - j))
    pltpu.make_async_copy(weights, left, left_sem).start()
    for b in range(n):
        @pl.when(slots[b] < NNB)
        def _():
            for copy in load([(refs[i], p) for i, p in where[b]], right.at[b], sem.at[b]):
                copy.start()

    if first:
        result[0] = jnp.zeros((BS, BS), jnp.bfloat16)
        for s in range(NNB):
            @pl.when(s >= counts[0])
            def _():
                pltpu.make_async_copy(result.at[0], out.at[s], out_sem.at[0]).start()
        for s in range(NNB):
            @pl.when(s >= counts[0])
            def _():
                pltpu.make_async_copy(result.at[0], out.at[s], out_sem.at[0]).wait()
    pltpu.make_async_copy(weights, left, left_sem).wait()
    for b in range(n):
        @pl.when(slots[b] < NNB)
        def _():
            for copy in load([(refs[i], p) for i, p in where[b]], right.at[b], sem.at[b]):
                copy.wait()
            multiply(left, right.at[b], result.at[b])
            pltpu.make_async_copy(result.at[b], out.at[slots[b]], out_sem.at[b]).start()
    for b in range(n):
        @pl.when(slots[b] < NNB)
        def _():
            pltpu.make_async_copy(result.at[b], out.at[slots[b]], out_sem.at[b]).wait()


def ask_kernel(blocks, where, near, far, *rest):
    n = len(blocks)
    refs, rest = rest[: n_arrays(where)], rest[n_arrays(where) :]
    outs, (left, right, left_sem, sem) = rest[:-4], rest[-4:]
    core, j, v = place(*blocks[0])
    alike = all(t == 1 for t, _ in blocks)
    if alike:
        use_near = jnp.where(core == 0, v > j, v < j)

        @pl.when(use_near)
        def _():
            for copy in load_mirrored(near, left.at[0], left_sem):
                copy.start()

        @pl.when(jnp.logical_not(use_near))
        def _():
            for copy in load_mirrored(far, left.at[0], left_sem):
                copy.start()
    else:
        for copy in load_mirrored(near, left.at[0], left_sem) + load_mirrored(far, left.at[1], left_sem):
            copy.start()
    for b in range(n):
        for copy in load([(refs[i], p) for i, p in where[b]], right.at[b], sem.at[b]):
            copy.start()
    for copy in load_mirrored(near, left.at[0], left_sem):
        copy.wait()
    if not alike:
        for copy in load_mirrored(far, left.at[1], left_sem):
            copy.wait()
    for b in range(n):
        for copy in load([(refs[i], p) for i, p in where[b]], right.at[b], sem.at[b]):
            copy.wait()
        _, _, v = place(*blocks[b])
        chosen = 0 if alike else jnp.where(jnp.where(core == 0, v > j, v < j), 0, 1)
        multiply(left.at[chosen], right.at[b], outs[0].at[b] if alike else outs[b])


def gather_kernel(steps, where, neighbours, counts, *rest):
    n = len(steps)
    refs, (_, out, held, sem, out_sem) = rest[:-5], rest[-5:]
    sources = [refs[i] if p is None else refs[i].at[p] for i, p in where]
    for i in range(n):
        pltpu.make_async_copy(sources[i], held.at[i], sem.at[i]).start()
    slots = []
    for i, (t, r) in enumerate(steps):
        slots.append(result_slot(neighbours, counts, t, r, True))
        pltpu.make_async_copy(sources[i], held.at[i], sem.at[i]).wait()

        @pl.when(slots[i] < NNB)
        def _():
            pltpu.make_async_copy(held.at[i], out.at[slots[i]], out_sem.at[i]).start()

    for i in range(n):
        @pl.when(slots[i] < NNB)
        def _():
            pltpu.make_async_copy(held.at[i], out.at[slots[i]], out_sem.at[i]).wait()


ANY = pl.BlockSpec(memory_space=pl.ANY)
SMEM = pl.BlockSpec(memory_space=pltpu.SMEM)
VMEM = pl.BlockSpec(memory_space=pltpu.VMEM)
OUT = jax.ShapeDtypeStruct((NNB, BS, BS), jnp.bfloat16)
RESULT = jax.ShapeDtypeStruct((BS, BS), jnp.bfloat16)
PAIR = jax.ShapeDtypeStruct((2, BS, KS), jnp.bfloat16)
WHOLE = jax.ShapeDtypeStruct((BS, STATES), jnp.bfloat16)
BLOCK = pltpu.VMEM((BS, STATES), jnp.bfloat16)


def cost(n):
    return pl.CostEstimate(flops=n * 2 * BS * BS * STATES, bytes_accessed=n * 9 * BS * BS, transcendentals=0)


def limit(mib):
    return pltpu.CompilerParams(vmem_limit_bytes=mib << 20)


def pick(block_order, coeffs):
    return pl.pallas_call(
        pick_kernel,
        out_shape=[PAIR] * 4,
        in_specs=[SMEM, ANY],
        out_specs=[VMEM] * 4,
        scratch_shapes=[pltpu.SemaphoreType.DMA],
        compiler_params=limit(8),
        name="pick",
    )(block_order, coeffs)


def distinct(blocks):
    arrays, where = [], []
    for parts in blocks:
        row = []
        for array, position in parts:
            n = next((i for i, other in enumerate(arrays) if other is array), len(arrays))
            if n == len(arrays):
                arrays.append(array)
            row.append((n, position))
        where.append(tuple(row))
    return arrays, tuple(where)


def weigh(occupations, parts):
    arrays, where = distinct([parts])
    return pl.pallas_call(
        functools.partial(weigh_kernel, where),
        out_shape=WHOLE,
        in_specs=[VMEM] + [ANY] * len(arrays),
        out_specs=VMEM,
        scratch_shapes=[BLOCK, pltpu.SemaphoreType.DMA],
        compiler_params=limit(12),
        name="weigh",
    )(occupations, *arrays)


def own_products(blocks, neighbours, counts, weights, parts, out):
    first = out is None
    extra = [] if first else [out]
    arrays, where = distinct(parts)
    m, n = len(arrays), len(blocks)
    return pl.pallas_call(
        functools.partial(own_kernel, blocks, first, where),
        out_shape=OUT,
        in_specs=[SMEM, SMEM] + [ANY] * (1 + m + len(extra)),
        out_specs=ANY,
        scratch_shapes=[
            BLOCK, pltpu.VMEM((n, BS, STATES), jnp.bfloat16), pltpu.VMEM((n, BS, BS), jnp.bfloat16),
            pltpu.SemaphoreType.DMA, pltpu.SemaphoreType.DMA((n,)), pltpu.SemaphoreType.DMA((n,)),
        ],
        input_output_aliases={} if first else {3 + m: 0},
        cost_estimate=cost(n),
        compiler_params=limit(20),
        name="own_products",
    )(neighbours, counts, weights, *arrays, *extra)


def ask_products(blocks, near, far, parts):
    arrays, where = distinct(parts)
    n = len(blocks)
    alike = all(t == 1 for t, _ in blocks)
    return pl.pallas_call(
        functools.partial(ask_kernel, blocks, where),
        out_shape=jax.ShapeDtypeStruct((n, BS, BS), jnp.bfloat16) if alike else [RESULT] * n,
        in_specs=[ANY] * (2 + len(arrays)),
        out_specs=VMEM if alike else [VMEM] * n,
        scratch_shapes=[
            pltpu.VMEM((1 if alike else 2, BS, STATES), jnp.bfloat16),
            pltpu.VMEM((n, BS, STATES), jnp.bfloat16),
            pltpu.SemaphoreType.DMA, pltpu.SemaphoreType.DMA((n,)),
        ],
        cost_estimate=cost(n),
        compiler_params=limit(20),
        name="ask_products",
    )(near, far, *arrays)


def gather(steps, neighbours, counts, results, out):
    arrays, where = distinct([results])
    n = len(steps)
    return pl.pallas_call(
        functools.partial(gather_kernel, steps, where[0]),
        out_shape=OUT,
        in_specs=[SMEM, SMEM] + [ANY] * (len(arrays) + 1),
        out_specs=ANY,
        scratch_shapes=[
            pltpu.VMEM((n, BS, BS), jnp.bfloat16),
            pltpu.SemaphoreType.DMA((n,)), pltpu.SemaphoreType.DMA((n,)),
        ],
        input_output_aliases={2 + len(arrays): 0},
        compiler_params=limit(8),
        name="place_results",
    )(neighbours, counts, *arrays, out)


def shards(coeffs, occupations, block_order, neighbours, counts):
    local = pick(block_order, coeffs.reshape(COLS, BS, KS))
    held = {("O", 0, "A"): local[0], ("O", 0, "Y"): local[1], ("O", 1, "A"): local[2], ("O", 1, "Y"): local[3]}
    up, down, far_up = {}, {}, {}
    for t in range(2):
        for part in "AY":
            held["P", t, part] = send(held["O", 1 - t, part], move_route(1, 0))
    for key in [(x, t, part) for t in range(2) for x in "OP" for part in "AY"]:
        up[key] = send(held[key], move_route(0, 1))
        down[key] = send(held[key], move_route(0, -1))
        if key[1:] == (1, "Y"):
            other = far_up["P" if key[0] == "O" else "O", 0, "Y"]
            far_up[key] = send(other, move_route(1, 0))
        else:
            far_up[key] = send(up[key], move_route(0, 1))

    own_at = {2: ("A", 0), 1: ("A", 1), 3: ("Y", 0), 0: ("Y", 1)}

    def parts_of(t, r):
        parts = []
        for x in "OP":
            for table, shift in ((held, 0), (up, 1), (far_up, 2), (down, -1)):
                part, position = own_at[(r + shift) % 4]
                parts.append((table[x, t, part], position))
        return parts

    weights = weigh(occupations.reshape(COLS, KS), parts_of(0, 0))
    near = send(weights, swap_route())
    far = send(weights, edge_route())
    out = own_products(((0, 0),), neighbours, counts, weights, [parts_of(0, 0)], None)

    half = ((0, 3), (0, 1), (0, 2))
    parts = [parts_of(*b) for b in half]
    out = own_products(half, neighbours, counts, weights, parts, out)
    answers = ask_products(half, near, far, parts)
    back = [(send(a, result_route(*b)), None) for a, b in zip(answers, half)]
    early, late = ((1, 0), (1, 1)), ((1, 3), (1, 2))
    for pair in (early, late):
        parts = [parts_of(*b) for b in pair]
        answer = ask_products(pair, near, far, parts)
        answer = send(answer, result_route(*pair[0]))
        back += [(answer, 0), (answer, 1)]
        out = own_products(pair, neighbours, counts, weights, parts, out)
    out = gather(half + early, neighbours, counts, back[:5], out)
    out = gather(late, neighbours, counts, back[5:], out)
    return out[None]


def solution(mesh):
    return jax.shard_map(
        shards,
        mesh=mesh,
        in_specs=(P("row", "col"), P(), P(), P(("row", "col"), None), P(("row", "col"))),
        out_specs=P(("row", "col"), None, None, None),
        check_vma=False,
    )
```

profile of v0, /device:TPU:9, one launch (start us, length us, event | category | flops | bytes accessed | tf_op | source)
XLA Modules:
  0.0 204.3 jit_solution(11399902062750105784)
XLA Ops:
  0.0 1.6 copy-done.6
  1.6 0.7 copy-done.8
  2.2 1.9 pick.1
  4.1 2.8 %collective-permute-start.4 = (bf16[2,512,256]{2,1,0:T(8,128)(2,1)}, bf16[2,512,256]{2,1,0:T(8,128)(2,1)}, u32[]{:S(2)}, u32[]{:S(2)}) collective-permute-start(bf16[2,512,256]{2,1,0:T(8,128)(2,1)} %get-tuple-element.15.rest_8_), channel_id=1, source_target_pairs={{4,0},{5,1},{6,2},{7,3},{0,4},{1,5},{2,6},{3,7},{12,8},{13,9},{14,... | collective-permute-start | bytes 1572872 | tf_op jit(solution)/shard_map/ppermute | solution.py:74
  7.0 0.2 collective-permute-start.3
  7.2 3.8 %collective-permute-start = (bf16[2,512,256]{2,1,0:T(8,128)(2,1)}, bf16[2,512,256]{2,1,0:T(8,128)(2,1)S(1)}, u32[]{:S(2)}, u32[]{:S(2)}) collective-permute-start(bf16[2,512,256]{2,1,0:T(8,128)(2,1)} %get-tuple-element.13.rest_8_), channel_id=1, source_target_pairs={{3,0},{0,1},{1,2},{2,3},{7,4},{4,5},{5,6},{6,7},{9,8},{10,9},{11,1... | collective-permute-start | bytes 1572872 | tf_op jit(solution)/shard_map/ppermute | solution.py:74
  11.0 7.9 %collective-permute-done.4.rest_12_ = bf16[2,512,256]{2,1,0:T(8,128)(2,1)} collective-permute-done((bf16[2,512,256]{2,1,0:T(8,128)(2,1)}, bf16[2,512,256]{2,1,0:T(8,128)(2,1)}, u32[]{:S(2)}, u32[]{:S(2)}) %collective-permute-start.4) | collective-permute-done | bytes 524320 | tf_op jit(solution)/shard_map/ppermute | solution.py:74
  18.9 3.8 %collective-permute-start.5 = (bf16[2,512,256]{2,1,0:T(8,128)(2,1)}, bf16[2,512,256]{2,1,0:T(8,128)(2,1)S(1)}, u32[]{:S(2)}, u32[]{:S(2)}) collective-permute-start(bf16[2,512,256]{2,1,0:T(8,128)(2,1)} %collective-permute-done.4.rest_12_), channel_id=1, source_target_pairs={{3,0},{0,1},{1,2},{2,3},{7,4},{4,5},{5,6},{6,7},{9,8},{10,9},{11,1... | collective-permute-start | bytes 1572872 | tf_op jit(solution)/shard_map/ppermute | solution.py:74
  22.6 2.7 %collective-permute-start.23 = (bf16[2,512,256]{2,1,0:T(8,128)(2,1)S(1)}, bf16[2,512,256]{2,1,0:T(8,128)(2,1)}, u32[]{:S(2)}, u32[]{:S(2)}) collective-permute-start(bf16[2,512,256]{2,1,0:T(8,128)(2,1)S(1)} %get-tuple-element.12.rest_0_), channel_id=1, source_target_pairs={{3,0},{0,1},{1,2},{2,3},{7,4},{4,5},{5,6},{6,7},{9,8},{10,9},{11,1... | collective-permute-start | bytes 1572872 | tf_op jit(solution)/shard_map/ppermute | solution.py:74
  25.3 4.7 %collective-permute-done.3.rest_4_ = bf16[2,512,256]{2,1,0:T(8,128)(2,1)S(1)} collective-permute-done((bf16[2,512,256]{2,1,0:T(8,128)(2,1)}, bf16[2,512,256]{2,1,0:T(8,128)(2,1)S(1)}, u32[]{:S(2)}, u32[]{:S(2)}) %collective-permute-start.3) | collective-permute-done | bytes 524320 | tf_op jit(solution)/shard_map/ppermute | solution.py:74
  30.0 1.6 collective-permute-start.7
  31.6 2.1 %collective-permute-start.1 = (bf16[2,512,256]{2,1,0:T(8,128)(2,1)S(1)}, bf16[2,512,256]{2,1,0:T(8,128)(2,1)S(1)}, u32[]{:S(2)}, u32[]{:S(2)}) collective-permute-start(bf16[2,512,256]{2,1,0:T(8,128)(2,1)S(1)} %collective-permute-done.rest_1_.rest_9_), channel_id=1, source_target_pairs={{3,0},{0,1},{1,2},{2,3},{7,4},{4,5},{5,6},{6,7},{9,8},{10,9},{11,1... | collective-permute-start | bytes 1572872 | tf_op jit(solution)/shard_map/ppermute | solution.py:74
  33.8 1.5 collective-permute-start.6
  35.2 2.2 %collective-permute-done.2.rest_3_.rest_11_ = bf16[2,512,256]{2,1,0:T(8,128)(2,1)S(1)} collective-permute-done((bf16[2,512,256]{2,1,0:T(8,128)(2,1)S(1)}, bf16[2,512,256]{2,1,0:T(8,128)(2,1)S(1)}, u32[]{:S(2)}, u32[]{:S(2)}) %collective-permute-start.2) | collective-permute-done | bytes 524320 | tf_op jit(solution)/shard_map/ppermute | solution.py:74
  37.4 2.7 %collective-permute-start.16 = (bf16[2,512,256]{2,1,0:T(8,128)(2,1)}, bf16[2,512,256]{2,1,0:T(8,128)(2,1)}, u32[]{:S(2)}, u32[]{:S(2)}) collective-permute-start(bf16[2,512,256]{2,1,0:T(8,128)(2,1)} %get-tuple-element.13.rest_8_), channel_id=1, source_target_pairs={{4,0},{5,1},{6,2},{7,3},{0,4},{1,5},{2,6},{3,7},{12,8},{13,9},{14,... | collective-permute-start | bytes 1572872 | tf_op jit(solution)/shard_map/ppermute | solution.py:74
  40.1 2.8 %collective-permute-done.23.rest_1_ = bf16[2,512,256]{2,1,0:T(8,128)(2,1)} collective-permute-done((bf16[2,512,256]{2,1,0:T(8,128)(2,1)S(1)}, bf16[2,512,256]{2,1,0:T(8,128)(2,1)}, u32[]{:S(2)}, u32[]{:S(2)}) %collective-permute-start.23) | collective-permute-done | bytes 524320 | tf_op jit(solution)/shard_map/ppermute | solution.py:74
  42.9 2.7 %collective-permute-start.14 = (bf16[2,512,256]{2,1,0:T(8,128)(2,1)S(1)}, bf16[2,512,256]{2,1,0:T(8,128)(2,1)}, u32[]{:S(2)}, u32[]{:S(2)}) collective-permute-start(bf16[2,512,256]{2,1,0:T(8,128)(2,1)S(1)} %get-tuple-element.12.rest_0_), channel_id=1, source_target_pairs={{4,0},{5,1},{6,2},{7,3},{0,4},{1,5},{2,6},{3,7},{12,8},{13,9},{14,... | collective-permute-start | bytes 1572872 | tf_op jit(solution)/shard_map/ppermute | solution.py:74
  45.6 3.1 %collective-permute-done.7.rest_7_.rest_15_ = bf16[2,512,256]{2,1,0:T(8,128)(2,1)S(1)} collective-permute-done((bf16[2,512,256]{2,1,0:T(8,128)(2,1)S(1)}, bf16[2,512,256]{2,1,0:T(8,128)(2,1)S(1)}, u32[]{:S(2)}, u32[]{:S(2)}) %collective-permute-start.7) | collective-permute-done | bytes 524320 | tf_op jit(solution)/shard_map/ppermute | solution.py:74
  48.7 0.3 collective-permute-start.11
  49.0 2.4 %collective-permute-done.1.rest_2_ = bf16[2,512,256]{2,1,0:T(8,128)(2,1)S(1)} collective-permute-done((bf16[2,512,256]{2,1,0:T(8,128)(2,1)S(1)}, bf16[2,512,256]{2,1,0:T(8,128)(2,1)S(1)}, u32[]{:S(2)}, u32[]{:S(2)}) %collective-permute-start.1) | collective-permute-done | bytes 524320 | tf_op jit(solution)/shard_map/ppermute | solution.py:74
  51.4 0.8 copy-done
  52.2 0.4 collective-permute-start.32
  52.6 4.5 %collective-permute-done.6.rest_6_ = bf16[2,512,256]{2,1,0:T(8,128)(2,1)S(1)} collective-permute-done((bf16[2,512,256]{2,1,0:T(8,128)(2,1)S(1)}, bf16[2,512,256]{2,1,0:T(8,128)(2,1)S(1)}, u32[]{:S(2)}, u32[]{:S(2)}) %collective-permute-start.6) | collective-permute-done | bytes 524320 | tf_op jit(solution)/shard_map/ppermute | solution.py:74
  57.0 0.8 copy-done.3
  57.8 3.5 %collective-permute-start.10 = (bf16[2,512,256]{2,1,0:T(8,128)(2,1)}, bf16[2,512,256]{2,1,0:T(8,128)(2,1)}, u32[]{:S(2)}, u32[]{:S(2)}) collective-permute-start(bf16[2,512,256]{2,1,0:T(8,128)(2,1)} %get-tuple-element.14.rest_0_), channel_id=1, source_target_pairs={{3,0},{0,1},{1,2},{2,3},{7,4},{4,5},{5,6},{6,7},{9,8},{10,9},{11,1... | collective-permute-start | bytes 1572872 | tf_op jit(solution)/shard_map/ppermute | solution.py:74
  61.3 0.7 reshape.6.occupations
  62.0 1.0 copy-done.1
  63.1 1.0 copy-done.4
  64.1 0.8 weigh.1.weights
  64.9 3.2 %collective-permute-start.8 = (bf16[512,2048]{1,0:T(8,128)(2,1)S(1)}, bf16[512,2048]{1,0:T(8,128)(2,1)S(1)}, u32[]{:S(2)}, u32[]{:S(2)}) collective-permute-start(bf16[512,2048]{1,0:T(8,128)(2,1)S(1)} %weigh.1.weights), channel_id=1, source_target_pairs={{0,8},{1,9},{2,10},{3,11},{4,12},{5,13},{6,14},{7,15},{8,0},{9,1},... | collective-permute-start | bytes 6291464 | tf_op jit(solution)/shard_map/ppermute | solution.py:74
  68.1 3.2 %collective-permute-start.9 = (bf16[512,2048]{1,0:T(8,128)(2,1)S(1)}, bf16[512,2048]{1,0:T(8,128)(2,1)S(1)}, u32[]{:S(2)}, u32[]{:S(2)}) collective-permute-start(bf16[512,2048]{1,0:T(8,128)(2,1)S(1)} %weigh.1.weights), channel_id=1, source_target_pairs={{8,16},{9,17},{10,18},{11,19},{12,20},{13,21},{14,22},{15,23},{16,... | collective-permute-start | bytes 6291464 | tf_op jit(solution)/shard_map/ppermute | solution.py:74
  71.3 3.0 %collective-permute-start.20 = (bf16[2,512,256]{2,1,0:T(8,128)(2,1)S(1)}, bf16[2,512,256]{2,1,0:T(8,128)(2,1)S(1)}, u32[]{:S(2)}, u32[]{:S(2)}) collective-permute-start(bf16[2,512,256]{2,1,0:T(8,128)(2,1)S(1)} %collective-permute-done.3.rest_4_), channel_id=1, source_target_pairs={{3,0},{0,1},{1,2},{2,3},{7,4},{4,5},{5,6},{6,7},{9,8},{10,9},{11,1... | collective-permute-start | bytes 1572872 | tf_op jit(solution)/shard_map/ppermute | solution.py:74
  74.4 0.1 collective-permute-start.24
  74.4 2.7 %collective-permute-start.17 = (bf16[2,512,256]{2,1,0:T(8,128)(2,1)}, bf16[2,512,256]{2,1,0:T(8,128)(2,1)S(1)}, u32[]{:S(2)}, u32[]{:S(2)}) collective-permute-start(bf16[2,512,256]{2,1,0:T(8,128)(2,1)} %collective-permute-done.16.rest_10_), channel_id=1, source_target_pairs={{3,0},{0,1},{1,2},{2,3},{7,4},{4,5},{5,6},{6,7},{9,8},{10,9},{11,1... | collective-permute-start | bytes 1572872 | tf_op jit(solution)/shard_map/ppermute | solution.py:74
  77.1 3.3 %collective-permute-done.20.rest_5_ = bf16[2,512,256]{2,1,0:T(8,128)(2,1)S(1)} collective-permute-done((bf16[2,512,256]{2,1,0:T(8,128)(2,1)S(1)}, bf16[2,512,256]{2,1,0:T(8,128)(2,1)S(1)}, u32[]{:S(2)}, u32[]{:S(2)}) %collective-permute-start.20) | collective-permute-done | bytes 524320 | tf_op jit(solution)/shard_map/ppermute | solution.py:74
  80.5 6.7 %collective-permute-done.24.rest_10_ = bf16[2,512,256]{2,1,0:T(8,128)(2,1)S(1)} collective-permute-done((bf16[2,512,256]{2,1,0:T(8,128)(2,1)}, bf16[2,512,256]{2,1,0:T(8,128)(2,1)S(1)}, u32[]{:S(2)}, u32[]{:S(2)}) %collective-permute-start.24) | collective-permute-done | bytes 524320 | tf_op jit(solution)/shard_map/ppermute | solution.py:74
  87.2 3.3 %collective-permute-start.12 = (bf16[2,512,256]{2,1,0:T(8,128)(2,1)}, bf16[2,512,256]{2,1,0:T(8,128)(2,1)S(1)}, u32[]{:S(2)}, u32[]{:S(2)}) collective-permute-start(bf16[2,512,256]{2,1,0:T(8,128)(2,1)} %collective-permute-done.11.rest_1_), channel_id=1, source_target_pairs={{3,0},{0,1},{1,2},{2,3},{7,4},{4,5},{5,6},{6,7},{9,8},{10,9},{11,1... | collective-permute-start | bytes 1572872 | tf_op jit(solution)/shard_map/ppermute | solution.py:74
  90.5 6.9 %collective-permute-done.17.rest_5_ = bf16[2,512,256]{2,1,0:T(8,128)(2,1)S(1)} collective-permute-done((bf16[2,512,256]{2,1,0:T(8,128)(2,1)}, bf16[2,512,256]{2,1,0:T(8,128)(2,1)S(1)}, u32[]{:S(2)}, u32[]{:S(2)}) %collective-permute-start.17) | collective-permute-done | bytes 524320 | tf_op jit(solution)/shard_map/ppermute | solution.py:74
  97.4 3.1 %collective-permute-start.21 = (bf16[2,512,256]{2,1,0:T(8,128)(2,1)S(1)}, bf16[2,512,256]{2,1,0:T(8,128)(2,1)S(1)}, u32[]{:S(2)}, u32[]{:S(2)}) collective-permute-start(bf16[2,512,256]{2,1,0:T(8,128)(2,1)S(1)} %collective-permute-done.20.rest_5_), channel_id=1, source_target_pairs={{3,0},{0,1},{1,2},{2,3},{7,4},{4,5},{5,6},{6,7},{9,8},{10,9},{11,1... | collective-permute-start | bytes 1572872 | tf_op jit(solution)/shard_map/ppermute | solution.py:74
  100.6 0.0 collective-permute-start.18
  100.6 2.4 %collective-permute-done.12.rest_2_ = bf16[2,512,256]{2,1,0:T(8,128)(2,1)S(1)} collective-permute-done((bf16[2,512,256]{2,1,0:T(8,128)(2,1)}, bf16[2,512,256]{2,1,0:T(8,128)(2,1)S(1)}, u32[]{:S(2)}, u32[]{:S(2)}) %collective-permute-start.12) | collective-permute-done | bytes 524320 | tf_op jit(solution)/shard_map/ppermute | solution.py:74
  103.1 2.3 %collective-permute-start.25 = (bf16[2,512,256]{2,1,0:T(8,128)(2,1)S(1)}, bf16[2,512,256]{2,1,0:T(8,128)(2,1)S(1)}, u32[]{:S(2)}, u32[]{:S(2)}) collective-permute-start(bf16[2,512,256]{2,1,0:T(8,128)(2,1)S(1)} %collective-permute-done.24.rest_10_), channel_id=1, source_target_pairs={{4,0},{5,1},{6,2},{7,3},{0,4},{1,5},{2,6},{3,7},{12,8},{13,9},{14,... | collective-permute-start | bytes 1572872 | tf_op jit(solution)/shard_map/ppermute | solution.py:74
  105.4 3.2 %collective-permute-done.21.rest_14_ = bf16[2,512,256]{2,1,0:T(8,128)(2,1)S(1)} collective-permute-done((bf16[2,512,256]{2,1,0:T(8,128)(2,1)S(1)}, bf16[2,512,256]{2,1,0:T(8,128)(2,1)S(1)}, u32[]{:S(2)}, u32[]{:S(2)}) %collective-permute-start.21) | collective-permute-done | bytes 524320 | tf_op jit(solution)/shard_map/ppermute | solution.py:74
  108.6 2.3 %collective-permute-start.22 = (bf16[2,512,256]{2,1,0:T(8,128)(2,1)S(1)}, bf16[2,512,256]{2,1,0:T(8,128)(2,1)S(1)}, u32[]{:S(2)}, u32[]{:S(2)}) collective-permute-start(bf16[2,512,256]{2,1,0:T(8,128)(2,1)S(1)} %collective-permute-done.21.rest_14_), channel_id=1, source_target_pairs={{4,0},{5,1},{6,2},{7,3},{0,4},{1,5},{2,6},{3,7},{12,8},{13,9},{14,... | collective-permute-start | bytes 1572872 | tf_op jit(solution)/shard_map/ppermute | solution.py:74
  110.9 3.3 %collective-permute-done.18.rest_6_ = bf16[2,512,256]{2,1,0:T(8,128)(2,1)S(1)} collective-permute-done((bf16[2,512,256]{2,1,0:T(8,128)(2,1)S(1)}, bf16[2,512,256]{2,1,0:T(8,128)(2,1)S(1)}, u32[]{:S(2)}, u32[]{:S(2)}) %collective-permute-start.18) | collective-permute-done | bytes 524320 | tf_op jit(solution)/shard_map/ppermute | solution.py:74
  114.2 16.3 %collective-permute-done.25.rest_11_ = bf16[2,512,256]{2,1,0:T(8,128)(2,1)S(1)} collective-permute-done((bf16[2,512,256]{2,1,0:T(8,128)(2,1)S(1)}, bf16[2,512,256]{2,1,0:T(8,128)(2,1)S(1)}, u32[]{:S(2)}, u32[]{:S(2)}) %collective-permute-start.25) | collective-permute-done | bytes 524320 | tf_op jit(solution)/shard_map/ppermute | solution.py:74
  130.5 3.0 %collective-permute-start.15 = (bf16[2,512,256]{2,1,0:T(8,128)(2,1)}, bf16[2,512,256]{2,1,0:T(8,128)(2,1)S(1)}, u32[]{:S(2)}, u32[]{:S(2)}) collective-permute-start(bf16[2,512,256]{2,1,0:T(8,128)(2,1)} %collective-permute-done.14.rest_4_), channel_id=1, source_target_pairs={{3,0},{0,1},{1,2},{2,3},{7,4},{4,5},{5,6},{6,7},{9,8},{10,9},{11,1... | collective-permute-start | bytes 1572872 | tf_op jit(solution)/shard_map/ppermute | solution.py:74
  133.4 8.3 %collective-permute-done.22.rest_9_ = bf16[2,512,256]{2,1,0:T(8,128)(2,1)S(1)} collective-permute-done((bf16[2,512,256]{2,1,0:T(8,128)(2,1)S(1)}, bf16[2,512,256]{2,1,0:T(8,128)(2,1)S(1)}, u32[]{:S(2)}, u32[]{:S(2)}) %collective-permute-start.22) | collective-permute-done | bytes 524320 | tf_op jit(solution)/shard_map/ppermute | solution.py:74
  141.7 0.4 collective-permute-start.27
  142.1 3.4 %collective-permute-start.28 = (bf16[2,512,256]{2,1,0:T(8,128)(2,1)}, bf16[2,512,256]{2,1,0:T(8,128)(2,1)S(1)}, u32[]{:S(2)}, u32[]{:S(2)}) collective-permute-start(bf16[2,512,256]{2,1,0:T(8,128)(2,1)} %collective-permute-done.4.rest_12_), channel_id=1, source_target_pairs={{1,0},{2,1},{3,2},{0,3},{5,4},{6,5},{7,6},{4,7},{11,8},{8,9},{9,10... | collective-permute-start | bytes 1572872 | tf_op jit(solution)/shard_map/ppermute | solution.py:74
  146.2 4.8 %ask_products.5 = bf16[2,512,512]{2,1,0:T(8,128)(2,1)S(1)} custom-call(bf16[512,2048]{1,0:T(8,128)(2,1)S(1)} %collective-permute-done.8.near, bf16[512,2048]{1,0:T(8,128)(2,1)S(1)} %collective-permute-done.9.far, bf16[2,512,256]{2,1,0:T(8,128)(2,1)} %get-tuple-element.14.rest_0_, bf16[2,512,256]{2,1,0:T(8,128)(2,1)} %collective-permute-done.11.rest_1_, ...), custom_call_target="tpu_custom_call" | custom-call | flops 2147483648 | bytes 4718592 | tf_op jit(solution)/shard_map/ask_products/pallas_call | solution.py:352
  151.0 2.8 %collective-permute-start.34 = (bf16[2,512,512]{2,1,0:T(8,128)(2,1)S(1)}, bf16[2,512,512]{2,1,0:T(8,128)(2,1)S(1)}, u32[]{:S(2)}, u32[]{:S(2)}) collective-permute-start(bf16[2,512,512]{2,1,0:T(8,128)(2,1)S(1)} %ask_products.5), channel_id=1, source_target_pairs={{0,8},{1,9},{2,10},{3,11},{8,16},{9,17},{10,18},{11,19},{12,4},{13... | collective-permute-start | bytes 3145736 | tf_op jit(solution)/shard_map/ppermute | solution.py:74
  153.8 4.6 %ask_products.3 = bf16[2,512,512]{2,1,0:T(8,128)(2,1)S(1)} custom-call(bf16[512,2048]{1,0:T(8,128)(2,1)S(1)} %collective-permute-done.8.near, bf16[512,2048]{1,0:T(8,128)(2,1)S(1)} %collective-permute-done.9.far, bf16[2,512,256]{2,1,0:T(8,128)(2,1)} %get-tuple-element.14.rest_0_, bf16[2,512,256]{2,1,0:T(8,128)(2,1)} %collective-permute-done.10.rest_1_, ...), custom_call_target="tpu_custom_call" | custom-call | flops 2147483648 | bytes 4718592 | tf_op jit(solution)/shard_map/ask_products/pallas_call | solution.py:352
  158.4 2.6 %collective-permute-start.26 = (bf16[2,512,512]{2,1,0:T(8,128)(2,1)S(1)}, bf16[2,512,512]{2,1,0:T(8,128)(2,1)S(1)}, u32[]{:S(2)}, u32[]{:S(2)}) collective-permute-start(bf16[2,512,512]{2,1,0:T(8,128)(2,1)S(1)} %ask_products.3), channel_id=1, source_target_pairs={{0,8},{1,9},{2,10},{3,11},{8,16},{9,17},{10,18},{11,19},{12,4},{13... | collective-permute-start | bytes 3145736 | tf_op jit(solution)/shard_map/ppermute | solution.py:74
  161.0 3.4 %own_products.4.rest_16_ = bf16[15,512,512]{2,1,0:T(8,128)(2,1)} custom-call(s32[1,15]{1,0:T(1,128)S(1)} %copy-done.7, s32[1]{0:T(128)S(6)} %copy.16.counts, bf16[512,2048]{1,0:T(8,128)(2,1)S(1)} %weigh.1.weights, bf16[2,512,256]{2,1,0:T(8,128)(2,1)S(1)} %get-tuple-element.12.rest_0_, bf16[2,512,256]{2,1,0:T(8,128)(2,1)S(1)} %collective-permute-done.rest_1_.rest_9_, ...), custom_call_target="tpu_custom_call" | custom-call | flops 1073741824 | bytes 2359296 | tf_op jit(solution)/shard_map/own_products/pallas_call | solution.py:332
  164.5 6.3 %ask_products.4 = (bf16[512,512]{1,0:T(8,128)(2,1)S(1)}, bf16[512,512]{1,0:T(8,128)(2,1)S(1)}, bf16[512,512]{1,0:T(8,128)(2,1)S(1)}) custom-call(bf16[512,2048]{1,0:T(8,128)(2,1)S(1)} %collective-permute-done.8.near, bf16[512,2048]{1,0:T(8,128)(2,1)S(1)} %collective-permute-done.9.far, bf16[2,512,256]{2,1,0:T(8,128)(2,1)S(1)} %get-tuple-element.12.rest_0_, ...), custom_call_target="tpu_custom_call" | custom-call | flops 3221225472 | bytes 7077888 | tf_op jit(solution)/shard_map/ask_products/pallas_call | solution.py:352
  170.8 4.6 %collective-permute-start.29 = (bf16[512,512]{1,0:T(8,128)(2,1)S(1)}, bf16[512,512]{1,0:T(8,128)(2,1)S(1)}, u32[]{:S(2)}, u32[]{:S(2)}) collective-permute-start(bf16[512,512]{1,0:T(8,128)(2,1)S(1)} %get-tuple-element.16), channel_id=1, source_target_pairs={{0,8},{4,12},{8,16},{9,17},{10,18},{11,3},{12,20},{13,21},{14,22},... | collective-permute-start | bytes 1572872 | tf_op jit(solution)/shard_map/ppermute | solution.py:74
  175.4 2.3 %collective-permute-start.30 = (bf16[512,512]{1,0:T(8,128)(2,1)S(1)}, bf16[512,512]{1,0:T(8,128)(2,1)S(1)}, u32[]{:S(2)}, u32[]{:S(2)}) collective-permute-start(bf16[512,512]{1,0:T(8,128)(2,1)S(1)} %get-tuple-element.17), channel_id=1, source_target_pairs={{0,8},{1,9},{2,10},{4,12},{5,13},{6,14},{8,16},{9,1},{10,2},{11,3}... | collective-permute-start | bytes 1572872 | tf_op jit(solution)/shard_map/ppermute | solution.py:74
  177.7 3.6 %collective-permute-start.31 = (bf16[512,512]{1,0:T(8,128)(2,1)S(1)}, bf16[512,512]{1,0:T(8,128)(2,1)S(1)}, u32[]{:S(2)}, u32[]{:S(2)}) collective-permute-start(bf16[512,512]{1,0:T(8,128)(2,1)S(1)} %get-tuple-element.18), channel_id=1, source_target_pairs={{0,8},{1,9},{4,12},{5,13},{8,16},{9,17},{10,2},{11,3},{12,20},{13,... | collective-permute-start | bytes 1572872 | tf_op jit(solution)/shard_map/ppermute | solution.py:74
  181.4 7.1 %own_products.5.rest_12_ = bf16[15,512,512]{2,1,0:T(8,128)(2,1)} custom-call(s32[1,15]{1,0:T(1,128)S(1)} %copy-done.7, s32[1]{0:T(128)S(6)} %copy.16.counts, bf16[512,2048]{1,0:T(8,128)(2,1)S(1)} %weigh.1.weights, bf16[2,512,256]{2,1,0:T(8,128)(2,1)S(1)} %get-tuple-element.12.rest_0_, ...), custom_call_target="tpu_custom_call", output_to_operand_aliasing={{}: (19, {})} | custom-call | flops 3221225472 | bytes 7077888 | tf_op jit(solution)/shard_map/own_products/pallas_call | solution.py:332
  188.5 5.8 %own_products.6.rest_12_ = bf16[15,512,512]{2,1,0:T(8,128)(2,1)} custom-call(s32[1,15]{1,0:T(1,128)S(1)} %copy-done.7, s32[1]{0:T(128)S(6)} %copy.16.counts, bf16[512,2048]{1,0:T(8,128)(2,1)S(1)} %weigh.1.weights, bf16[2,512,256]{2,1,0:T(8,128)(2,1)} %get-tuple-element.14.rest_0_, ...), custom_call_target="tpu_custom_call", output_to_operand_aliasing={{}: (15, {})} | custom-call | flops 2147483648 | bytes 4718592 | tf_op jit(solution)/shard_map/own_products/pallas_call | solution.py:332
  194.3 5.7 %own_products.7.rest_4_ = bf16[15,512,512]{2,1,0:T(8,128)(2,1)} custom-call(s32[1,15]{1,0:T(1,128)S(1)} %copy-done.7, s32[1]{0:T(128)S(6)} %copy.16.counts, bf16[512,2048]{1,0:T(8,128)(2,1)S(1)} %weigh.1.weights, bf16[2,512,256]{2,1,0:T(8,128)(2,1)} %get-tuple-element.14.rest_0_, ...), custom_call_target="tpu_custom_call", output_to_operand_aliasing={{}: (15, {})} | custom-call | flops 2147483648 | bytes 4718592 | tf_op jit(solution)/shard_map/own_products/pallas_call | solution.py:332
  200.0 2.4 %place_results.2.rest_1_ = bf16[15,512,512]{2,1,0:T(8,128)(2,1)} custom-call(s32[1,15]{1,0:T(1,128)S(1)} %copy-done.7, s32[1]{0:T(128)S(6)} %copy.16.counts, bf16[512,512]{1,0:T(8,128)(2,1)S(1)} %collective-permute-done.29.rest_0_, bf16[512,512]{1,0:T(8,128)(2,1)S(1)} %collective-permute-done.30.rest_1_, ...), custom_call_target="tpu_custom_call", output_to_operand_aliasing={{}: (6, {})} | custom-call | tf_op jit(solution)/shard_map/place_results/pallas_call | solution.py:371
  202.4 1.7 place_results.3
  (36 shorter events, 0.1 us)
Async XLA Ops:
  0.0 1.6 copy-start.6
  1.6 0.7 copy-start.8
  4.1 14.7 %collective-permute-start.4 = (bf16[2,512,256]{2,1,0:T(8,128)(2,1)}, bf16[2,512,256]{2,1,0:T(8,128)(2,1)}, u32[]{:S(2)}, u32[]{:S(2)}) collective-permute-start(bf16[2,512,256]{2,1,0:T(8,128)(2,1)} %get-tuple-element.15.rest_8_), channel_id=1, source_target_pairs={{4,0},{5,1},{6,2},{7,3},{0,4},{1,5},{2,6},{3,7},{12,8},{13,9},{14,... | collective-permute-start | bytes 1572872 | tf_op jit(solution)/shard_map/ppermute | solution.py:74
  7.0 23.0 %collective-permute-start.3 = (bf16[2,512,256]{2,1,0:T(8,128)(2,1)}, bf16[2,512,256]{2,1,0:T(8,128)(2,1)S(1)}, u32[]{:S(2)}, u32[]{:S(2)}) collective-permute-start(bf16[2,512,256]{2,1,0:T(8,128)(2,1)} %get-tuple-element.14.rest_0_), channel_id=1, source_target_pairs={{4,0},{5,1},{6,2},{7,3},{0,4},{1,5},{2,6},{3,7},{12,8},{13,9},{14,... | collective-permute-start | bytes 1572872 | tf_op jit(solution)/shard_map/ppermute | solution.py:74
  7.2 24.4 %collective-permute-start = (bf16[2,512,256]{2,1,0:T(8,128)(2,1)}, bf16[2,512,256]{2,1,0:T(8,128)(2,1)S(1)}, u32[]{:S(2)}, u32[]{:S(2)}) collective-permute-start(bf16[2,512,256]{2,1,0:T(8,128)(2,1)} %get-tuple-element.13.rest_8_), channel_id=1, source_target_pairs={{3,0},{0,1},{1,2},{2,3},{7,4},{4,5},{5,6},{6,7},{9,8},{10,9},{11,1... | collective-permute-start | bytes 1572872 | tf_op jit(solution)/shard_map/ppermute | solution.py:74
  18.9 14.9 %collective-permute-start.5 = (bf16[2,512,256]{2,1,0:T(8,128)(2,1)}, bf16[2,512,256]{2,1,0:T(8,128)(2,1)S(1)}, u32[]{:S(2)}, u32[]{:S(2)}) collective-permute-start(bf16[2,512,256]{2,1,0:T(8,128)(2,1)} %collective-permute-done.4.rest_12_), channel_id=1, source_target_pairs={{3,0},{0,1},{1,2},{2,3},{7,4},{4,5},{5,6},{6,7},{9,8},{10,9},{11,1... | collective-permute-start | bytes 1572872 | tf_op jit(solution)/shard_map/ppermute | solution.py:74
  22.6 14.8 %collective-permute-start.2 = (bf16[2,512,256]{2,1,0:T(8,128)(2,1)S(1)}, bf16[2,512,256]{2,1,0:T(8,128)(2,1)S(1)}, u32[]{:S(2)}, u32[]{:S(2)}) collective-permute-start(bf16[2,512,256]{2,1,0:T(8,128)(2,1)S(1)} %get-tuple-element.12.rest_0_), channel_id=1, source_target_pairs={{1,0},{2,1},{3,2},{0,3},{5,4},{6,5},{7,6},{4,7},{11,8},{8,9},{9,10... | collective-permute-start | bytes 1572872 | tf_op jit(solution)/shard_map/ppermute | solution.py:74
  22.6 20.3 %collective-permute-start.23 = (bf16[2,512,256]{2,1,0:T(8,128)(2,1)S(1)}, bf16[2,512,256]{2,1,0:T(8,128)(2,1)}, u32[]{:S(2)}, u32[]{:S(2)}) collective-permute-start(bf16[2,512,256]{2,1,0:T(8,128)(2,1)S(1)} %get-tuple-element.12.rest_0_), channel_id=1, source_target_pairs={{3,0},{0,1},{1,2},{2,3},{7,4},{4,5},{5,6},{6,7},{9,8},{10,9},{11,1... | collective-permute-start | bytes 1572872 | tf_op jit(solution)/shard_map/ppermute | solution.py:74
  30.0 18.7 %collective-permute-start.7 = (bf16[2,512,256]{2,1,0:T(8,128)(2,1)S(1)}, bf16[2,512,256]{2,1,0:T(8,128)(2,1)S(1)}, u32[]{:S(2)}, u32[]{:S(2)}) collective-permute-start(bf16[2,512,256]{2,1,0:T(8,128)(2,1)S(1)} %collective-permute-done.3.rest_4_), channel_id=1, source_target_pairs={{1,0},{2,1},{3,2},{0,3},{5,4},{6,5},{7,6},{4,7},{11,8},{8,9},{9,10... | collective-permute-start | bytes 1572872 | tf_op jit(solution)/shard_map/ppermute | solution.py:74
  31.6 19.8 %collective-permute-start.1 = (bf16[2,512,256]{2,1,0:T(8,128)(2,1)S(1)}, bf16[2,512,256]{2,1,0:T(8,128)(2,1)S(1)}, u32[]{:S(2)}, u32[]{:S(2)}) collective-permute-start(bf16[2,512,256]{2,1,0:T(8,128)(2,1)S(1)} %collective-permute-done.rest_1_.rest_9_), channel_id=1, source_target_pairs={{3,0},{0,1},{1,2},{2,3},{7,4},{4,5},{5,6},{6,7},{9,8},{10,9},{11,1... | collective-permute-start | bytes 1572872 | tf_op jit(solution)/shard_map/ppermute | solution.py:74
  33.8 23.3 %collective-permute-start.6 = (bf16[2,512,256]{2,1,0:T(8,128)(2,1)S(1)}, bf16[2,512,256]{2,1,0:T(8,128)(2,1)S(1)}, u32[]{:S(2)}, u32[]{:S(2)}) collective-permute-start(bf16[2,512,256]{2,1,0:T(8,128)(2,1)S(1)} %collective-permute-done.5.rest_5_.rest_13_), channel_id=1, source_target_pairs={{3,0},{0,1},{1,2},{2,3},{7,4},{4,5},{5,6},{6,7},{9,8},{10,9},{11,1... | collective-permute-start | bytes 1572872 | tf_op jit(solution)/shard_map/ppermute | solution.py:74
  37.4 27.5 %collective-permute-start.16 = (bf16[2,512,256]{2,1,0:T(8,128)(2,1)}, bf16[2,512,256]{2,1,0:T(8,128)(2,1)}, u32[]{:S(2)}, u32[]{:S(2)}) collective-permute-start(bf16[2,512,256]{2,1,0:T(8,128)(2,1)} %get-tuple-element.13.rest_8_), channel_id=1, source_target_pairs={{4,0},{5,1},{6,2},{7,3},{0,4},{1,5},{2,6},{3,7},{12,8},{13,9},{14,... | collective-permute-start | bytes 1572872 | tf_op jit(solution)/shard_map/ppermute | solution.py:74
  42.9 25.3 %collective-permute-start.14 = (bf16[2,512,256]{2,1,0:T(8,128)(2,1)S(1)}, bf16[2,512,256]{2,1,0:T(8,128)(2,1)}, u32[]{:S(2)}, u32[]{:S(2)}) collective-permute-start(bf16[2,512,256]{2,1,0:T(8,128)(2,1)S(1)} %get-tuple-element.12.rest_0_), channel_id=1, source_target_pairs={{4,0},{5,1},{6,2},{7,3},{0,4},{1,5},{2,6},{3,7},{12,8},{13,9},{14,... | collective-permute-start | bytes 1572872 | tf_op jit(solution)/shard_map/ppermute | solution.py:74
  48.7 22.6 %collective-permute-start.11 = (bf16[2,512,256]{2,1,0:T(8,128)(2,1)}, bf16[2,512,256]{2,1,0:T(8,128)(2,1)}, u32[]{:S(2)}, u32[]{:S(2)}) collective-permute-start(bf16[2,512,256]{2,1,0:T(8,128)(2,1)} %get-tuple-element.15.rest_8_), channel_id=1, source_target_pairs={{3,0},{0,1},{1,2},{2,3},{7,4},{4,5},{5,6},{6,7},{9,8},{10,9},{11,1... | collective-permute-start | bytes 1572872 | tf_op jit(solution)/shard_map/ppermute | solution.py:74
  51.4 0.8 copy-start
  52.2 22.1 %collective-permute-start.32 = (bf16[2,512,256]{2,1,0:T(8,128)(2,1)}, bf16[2,512,256]{2,1,0:T(8,128)(2,1)}, u32[]{:S(2)}, u32[]{:S(2)}) collective-permute-start(bf16[2,512,256]{2,1,0:T(8,128)(2,1)} %get-tuple-element.14.rest_0_), channel_id=1, source_target_pairs={{1,0},{2,1},{3,2},{0,3},{5,4},{6,5},{7,6},{4,7},{11,8},{8,9},{9,10... | collective-permute-start | bytes 1572872 | tf_op jit(solution)/shard_map/ppermute | solution.py:74
  57.0 0.8 copy-start.3
  57.8 16.6 %collective-permute-start.10 = (bf16[2,512,256]{2,1,0:T(8,128)(2,1)}, bf16[2,512,256]{2,1,0:T(8,128)(2,1)}, u32[]{:S(2)}, u32[]{:S(2)}) collective-permute-start(bf16[2,512,256]{2,1,0:T(8,128)(2,1)} %get-tuple-element.14.rest_0_), channel_id=1, source_target_pairs={{3,0},{0,1},{1,2},{2,3},{7,4},{4,5},{5,6},{6,7},{9,8},{10,9},{11,1... | collective-permute-start | bytes 1572872 | tf_op jit(solution)/shard_map/ppermute | solution.py:74
  62.0 1.0 copy-start.1
  63.1 1.0 copy-start.4
  64.9 76.8 %collective-permute-start.8 = (bf16[512,2048]{1,0:T(8,128)(2,1)S(1)}, bf16[512,2048]{1,0:T(8,128)(2,1)S(1)}, u32[]{:S(2)}, u32[]{:S(2)}) collective-permute-start(bf16[512,2048]{1,0:T(8,128)(2,1)S(1)} %weigh.1.weights), channel_id=1, source_target_pairs={{0,8},{1,9},{2,10},{3,11},{4,12},{5,13},{6,14},{7,15},{8,0},{9,1},... | collective-permute-start | bytes 6291464 | tf_op jit(solution)/shard_map/ppermute | solution.py:74
  68.1 74.0 %collective-permute-start.9 = (bf16[512,2048]{1,0:T(8,128)(2,1)S(1)}, bf16[512,2048]{1,0:T(8,128)(2,1)S(1)}, u32[]{:S(2)}, u32[]{:S(2)}) collective-permute-start(bf16[512,2048]{1,0:T(8,128)(2,1)S(1)} %weigh.1.weights), channel_id=1, source_target_pairs={{8,16},{9,17},{10,18},{11,19},{12,20},{13,21},{14,22},{15,23},{16,... | collective-permute-start | bytes 6291464 | tf_op jit(solution)/shard_map/ppermute | solution.py:74
  71.3 9.1 %collective-permute-start.20 = (bf16[2,512,256]{2,1,0:T(8,128)(2,1)S(1)}, bf16[2,512,256]{2,1,0:T(8,128)(2,1)S(1)}, u32[]{:S(2)}, u32[]{:S(2)}) collective-permute-start(bf16[2,512,256]{2,1,0:T(8,128)(2,1)S(1)} %collective-permute-done.3.rest_4_), channel_id=1, source_target_pairs={{3,0},{0,1},{1,2},{2,3},{7,4},{4,5},{5,6},{6,7},{9,8},{10,9},{11,1... | collective-permute-start | bytes 1572872 | tf_op jit(solution)/shard_map/ppermute | solution.py:74
  74.4 12.9 %collective-permute-start.24 = (bf16[2,512,256]{2,1,0:T(8,128)(2,1)}, bf16[2,512,256]{2,1,0:T(8,128)(2,1)S(1)}, u32[]{:S(2)}, u32[]{:S(2)}) collective-permute-start(bf16[2,512,256]{2,1,0:T(8,128)(2,1)} %collective-permute-done.23.rest_1_), channel_id=1, source_target_pairs={{3,0},{0,1},{1,2},{2,3},{7,4},{4,5},{5,6},{6,7},{9,8},{10,9},{11,1... | collective-permute-start | bytes 1572872 | tf_op jit(solution)/shard_map/ppermute | solution.py:74
  74.4 23.0 %collective-permute-start.17 = (bf16[2,512,256]{2,1,0:T(8,128)(2,1)}, bf16[2,512,256]{2,1,0:T(8,128)(2,1)S(1)}, u32[]{:S(2)}, u32[]{:S(2)}) collective-permute-start(bf16[2,512,256]{2,1,0:T(8,128)(2,1)} %collective-permute-done.16.rest_10_), channel_id=1, source_target_pairs={{3,0},{0,1},{1,2},{2,3},{7,4},{4,5},{5,6},{6,7},{9,8},{10,9},{11,1... | collective-permute-start | bytes 1572872 | tf_op jit(solution)/shard_map/ppermute | solution.py:74
  80.5 20.1 %collective-permute-start.33 = (bf16[2,512,256]{2,1,0:T(8,128)(2,1)}, bf16[2,512,256]{2,1,0:T(8,128)(2,1)S(1)}, u32[]{:S(2)}, u32[]{:S(2)}) collective-permute-start(bf16[2,512,256]{2,1,0:T(8,128)(2,1)} %collective-permute-done.14.rest_4_), channel_id=1, source_target_pairs={{1,0},{2,1},{3,2},{0,3},{5,4},{6,5},{7,6},{4,7},{11,8},{8,9},{9,10... | collective-permute-start | bytes 1572872 | tf_op jit(solution)/shard_map/ppermute | solution.py:74
  87.2 15.8 %collective-permute-start.12 = (bf16[2,512,256]{2,1,0:T(8,128)(2,1)}, bf16[2,512,256]{2,1,0:T(8,128)(2,1)S(1)}, u32[]{:S(2)}, u32[]{:S(2)}) collective-permute-start(bf16[2,512,256]{2,1,0:T(8,128)(2,1)} %collective-permute-done.11.rest_1_), channel_id=1, source_target_pairs={{3,0},{0,1},{1,2},{2,3},{7,4},{4,5},{5,6},{6,7},{9,8},{10,9},{11,1... | collective-permute-start | bytes 1572872 | tf_op jit(solution)/shard_map/ppermute | solution.py:74
  97.4 11.1 %collective-permute-start.21 = (bf16[2,512,256]{2,1,0:T(8,128)(2,1)S(1)}, bf16[2,512,256]{2,1,0:T(8,128)(2,1)S(1)}, u32[]{:S(2)}, u32[]{:S(2)}) collective-permute-start(bf16[2,512,256]{2,1,0:T(8,128)(2,1)S(1)} %collective-permute-done.20.rest_5_), channel_id=1, source_target_pairs={{3,0},{0,1},{1,2},{2,3},{7,4},{4,5},{5,6},{6,7},{9,8},{10,9},{11,1... | collective-permute-start | bytes 1572872 | tf_op jit(solution)/shard_map/ppermute | solution.py:74
  100.6 13.6 %collective-permute-start.18 = (bf16[2,512,256]{2,1,0:T(8,128)(2,1)S(1)}, bf16[2,512,256]{2,1,0:T(8,128)(2,1)S(1)}, u32[]{:S(2)}, u32[]{:S(2)}) collective-permute-start(bf16[2,512,256]{2,1,0:T(8,128)(2,1)S(1)} %collective-permute-done.17.rest_5_), channel_id=1, source_target_pairs={{3,0},{0,1},{1,2},{2,3},{7,4},{4,5},{5,6},{6,7},{9,8},{10,9},{11,1... | collective-permute-start | bytes 1572872 | tf_op jit(solution)/shard_map/ppermute | solution.py:74
  103.1 27.4 %collective-permute-start.25 = (bf16[2,512,256]{2,1,0:T(8,128)(2,1)S(1)}, bf16[2,512,256]{2,1,0:T(8,128)(2,1)S(1)}, u32[]{:S(2)}, u32[]{:S(2)}) collective-permute-start(bf16[2,512,256]{2,1,0:T(8,128)(2,1)S(1)} %collective-permute-done.24.rest_10_), channel_id=1, source_target_pairs={{4,0},{5,1},{6,2},{7,3},{0,4},{1,5},{2,6},{3,7},{12,8},{13,9},{14,... | collective-permute-start | bytes 1572872 | tf_op jit(solution)/shard_map/ppermute | solution.py:74
  108.6 33.1 %collective-permute-start.22 = (bf16[2,512,256]{2,1,0:T(8,128)(2,1)S(1)}, bf16[2,512,256]{2,1,0:T(8,128)(2,1)S(1)}, u32[]{:S(2)}, u32[]{:S(2)}) collective-permute-start(bf16[2,512,256]{2,1,0:T(8,128)(2,1)S(1)} %collective-permute-done.21.rest_14_), channel_id=1, source_target_pairs={{4,0},{5,1},{6,2},{7,3},{0,4},{1,5},{2,6},{3,7},{12,8},{13,9},{14,... | collective-permute-start | bytes 1572872 | tf_op jit(solution)/shard_map/ppermute | solution.py:74
  114.2 36.8 %collective-permute-start.13 = (bf16[2,512,256]{2,1,0:T(8,128)(2,1)}, bf16[2,512,256]{2,1,0:T(8,128)(2,1)S(1)}, u32[]{:S(2)}, u32[]{:S(2)}) collective-permute-start(bf16[2,512,256]{2,1,0:T(8,128)(2,1)} %get-tuple-element.15.rest_8_), channel_id=1, source_target_pairs={{1,0},{2,1},{3,2},{0,3},{5,4},{6,5},{7,6},{4,7},{11,8},{8,9},{9,10... | collective-permute-start | bytes 1572872 | tf_op jit(solution)/shard_map/ppermute | solution.py:74
  130.5 23.4 %collective-permute-start.15 = (bf16[2,512,256]{2,1,0:T(8,128)(2,1)}, bf16[2,512,256]{2,1,0:T(8,128)(2,1)S(1)}, u32[]{:S(2)}, u32[]{:S(2)}) collective-permute-start(bf16[2,512,256]{2,1,0:T(8,128)(2,1)} %collective-permute-done.14.rest_4_), channel_id=1, source_target_pairs={{3,0},{0,1},{1,2},{2,3},{7,4},{4,5},{5,6},{6,7},{9,8},{10,9},{11,1... | collective-permute-start | bytes 1572872 | tf_op jit(solution)/shard_map/ppermute | solution.py:74
  141.7 12.1 %collective-permute-start.19 = (bf16[2,512,256]{2,1,0:T(8,128)(2,1)}, bf16[2,512,256]{2,1,0:T(8,128)(2,1)S(1)}, u32[]{:S(2)}, u32[]{:S(2)}) collective-permute-start(bf16[2,512,256]{2,1,0:T(8,128)(2,1)} %collective-permute-done.16.rest_10_), channel_id=1, source_target_pairs={{1,0},{2,1},{3,2},{0,3},{5,4},{6,5},{7,6},{4,7},{11,8},{8,9},{9,10... | collective-permute-start | bytes 1572872 | tf_op jit(solution)/shard_map/ppermute | solution.py:74
  141.7 22.8 %collective-permute-start.27 = (bf16[2,512,256]{2,1,0:T(8,128)(2,1)}, bf16[2,512,256]{2,1,0:T(8,128)(2,1)S(1)}, u32[]{:S(2)}, u32[]{:S(2)}) collective-permute-start(bf16[2,512,256]{2,1,0:T(8,128)(2,1)} %get-tuple-element.13.rest_8_), channel_id=1, source_target_pairs={{1,0},{2,1},{3,2},{0,3},{5,4},{6,5},{7,6},{4,7},{11,8},{8,9},{9,10... | collective-permute-start | bytes 1572872 | tf_op jit(solution)/shard_map/ppermute | solution.py:74
  142.1 22.4 %collective-permute-start.28 = (bf16[2,512,256]{2,1,0:T(8,128)(2,1)}, bf16[2,512,256]{2,1,0:T(8,128)(2,1)S(1)}, u32[]{:S(2)}, u32[]{:S(2)}) collective-permute-start(bf16[2,512,256]{2,1,0:T(8,128)(2,1)} %collective-permute-done.4.rest_12_), channel_id=1, source_target_pairs={{1,0},{2,1},{3,2},{0,3},{5,4},{6,5},{7,6},{4,7},{11,8},{8,9},{9,10... | collective-permute-start | bytes 1572872 | tf_op jit(solution)/shard_map/ppermute | solution.py:74
  151.0 10.0 %copy-start.2 = (bf16[2,512,256]{2,1,0:T(8,128)(2,1)S(1)}, bf16[2,512,256]{2,1,0:T(8,128)(2,1)}, u32[]{:S(2)}) copy-start(bf16[2,512,256]{2,1,0:T(8,128)(2,1)} %copy-done) | copy-start | bytes 1572868
  151.0 10.0 %copy-start.5 = (bf16[2,512,256]{2,1,0:T(8,128)(2,1)S(1)}, bf16[2,512,256]{2,1,0:T(8,128)(2,1)}, u32[]{:S(2)}) copy-start(bf16[2,512,256]{2,1,0:T(8,128)(2,1)} %copy-done.3) | copy-start | bytes 1572868
  151.0 10.0 %copy-start.7 = (s32[1,15]{1,0:T(1,128)S(1)}, s32[1,15]{1,0:T(1,128)}, u32[]{:S(2)}) copy-start(s32[1,15]{1,0:T(1,128)} %neighbours.11) | copy-start | bytes 184
  151.0 49.0 %collective-permute-start.34 = (bf16[2,512,512]{2,1,0:T(8,128)(2,1)S(1)}, bf16[2,512,512]{2,1,0:T(8,128)(2,1)S(1)}, u32[]{:S(2)}, u32[]{:S(2)}) collective-permute-start(bf16[2,512,512]{2,1,0:T(8,128)(2,1)S(1)} %ask_products.5), channel_id=1, source_target_pairs={{0,8},{1,9},{2,10},{3,11},{8,16},{9,17},{10,18},{11,19},{12,4},{13... | collective-permute-start | bytes 3145736 | tf_op jit(solution)/shard_map/ppermute | solution.py:74
  158.4 44.0 %collective-permute-start.26 = (bf16[2,512,512]{2,1,0:T(8,128)(2,1)S(1)}, bf16[2,512,512]{2,1,0:T(8,128)(2,1)S(1)}, u32[]{:S(2)}, u32[]{:S(2)}) collective-permute-start(bf16[2,512,512]{2,1,0:T(8,128)(2,1)S(1)} %ask_products.3), channel_id=1, source_target_pairs={{0,8},{1,9},{2,10},{3,11},{8,16},{9,17},{10,18},{11,19},{12,4},{13... | collective-permute-start | bytes 3145736 | tf_op jit(solution)/shard_map/ppermute | solution.py:74
  170.8 29.2 %collective-permute-start.29 = (bf16[512,512]{1,0:T(8,128)(2,1)S(1)}, bf16[512,512]{1,0:T(8,128)(2,1)S(1)}, u32[]{:S(2)}, u32[]{:S(2)}) collective-permute-start(bf16[512,512]{1,0:T(8,128)(2,1)S(1)} %get-tuple-element.16), channel_id=1, source_target_pairs={{0,8},{4,12},{8,16},{9,17},{10,18},{11,3},{12,20},{13,21},{14,22},... | collective-permute-start | bytes 1572872 | tf_op jit(solution)/shard_map/ppermute | solution.py:74
  175.4 24.6 %collective-permute-start.30 = (bf16[512,512]{1,0:T(8,128)(2,1)S(1)}, bf16[512,512]{1,0:T(8,128)(2,1)S(1)}, u32[]{:S(2)}, u32[]{:S(2)}) collective-permute-start(bf16[512,512]{1,0:T(8,128)(2,1)S(1)} %get-tuple-element.17), channel_id=1, source_target_pairs={{0,8},{1,9},{2,10},{4,12},{5,13},{6,14},{8,16},{9,1},{10,2},{11,3}... | collective-permute-start | bytes 1572872 | tf_op jit(solution)/shard_map/ppermute | solution.py:74
  177.7 22.3 %collective-permute-start.31 = (bf16[512,512]{1,0:T(8,128)(2,1)S(1)}, bf16[512,512]{1,0:T(8,128)(2,1)S(1)}, u32[]{:S(2)}, u32[]{:S(2)}) collective-permute-start(bf16[512,512]{1,0:T(8,128)(2,1)S(1)} %get-tuple-element.18), channel_id=1, source_target_pairs={{0,8},{1,9},{4,12},{5,13},{8,16},{9,17},{10,2},{11,3},{12,20},{13,... | collective-permute-start | bytes 1572872 | tf_op jit(solution)/shard_map/ppermute | solution.py:74
where the time goes:
time: 205 us; the launch traced here: 204 us
  waiting for transfers between devices  78 us (38%)
  starting transfers between devices  74.1 us (36%)
  Pallas kernels  44.4 us (22%)
  local copies, waits for them, and re-layouts  6.63 us (3%)
    ppermute x35, waiting for transfers between devices, send(): return lax.ppermute(value, AXES, route)  78 us
    ppermute x35, starting transfers between devices, send(): return lax.ppermute(value, AXES, route)  74.1 us
    pallas_call x4, Pallas kernels, own_products(): pl.pallas_call(functools.partial(own_kernel, blocks, first, where), out_s...  22 us
    pallas_call x3, Pallas kernels, ask_products(): pl.pallas_call(functools.partial(ask_kernel, blocks, where), out_shape=ja...  15.7 us
    unnamed x18, local copies, waits for them, and re-layouts  5.93 us
  transfers between devices with their start and end apart: 35, of which 15 were waited for; matrix products, arithmetic and copies ran while one was open for 0% of the time, Pallas kernels for 20%

commit v1 on v0

--- a/solution.py
+++ b/solution.py
@@ -47,21 +47,52 @@
     return (k + 1, 0) if core else (k - 1, 1)
 
 
+def in_plane(k, core):
+    return (k % 2 == 0) != (core == 0)
+
+
 def edge_route():
     pairs = []
     for k, c, x, z in devices():
         to, tc = partner_of(k, c)
-        if 0 <= to < 8:
+        if 0 <= to < 8 and in_plane(k, c):
             pairs.append((index(k, c, x, z), index(to, tc, x, z)))
     return pairs
 
 
-def result_route(t, r):
+def plane_routes():
+    first, second = [], []
+    for k, c, x, z in devices():
+        to, tc = partner_of(k, c)
+        if 0 <= to < 8 and not in_plane(k, c):
+            middle = index(2 * to - k, c, x, z)
+            first.append((index(k, c, x, z), middle))
+            second.append((middle, index(to, tc, x, z)))
+    return first, second
+
+
+def asks_near(core, xh):
+    return (core == 0) == (xh == 0)
+
+
+def across_route():
     pairs = []
     for k, c, x, z in devices():
-        j = x * 4 + z
-        v = (x ^ t) * 4 + (z + r * up_of(c)) % 4
-        if (v > j) != bool(c):
+        to, tc = partner_of(k, c)
+        if 0 <= to < 8 and asks_near(c, x):
+            pairs.append((index(k, c, x, z), index(to, tc, 1 - x, z)))
+    return pairs
+
+
+def near_route():
+    return [(index(k, c, x, z), index(k, 1 - c, x, z)) for k, c, x, z in devices() if asks_near(c, x)]
+
+
+def result_route(r):
+    pairs = []
+    for k, c, x, z in devices():
+        v = (z + r * up_of(c)) % 4
+        if (v > z) != bool(c):
             to, tc = k, 1 - c
         else:
             to, tc = partner_of(k, c)
@@ -117,9 +148,9 @@
 MIRROR = (0, 3, 2, 1, 4, 7, 6, 5)
 
 
-def load_mirrored(whole, target, sem):
+def load_mirrored(whole, target, sem, halves=0):
     return [
-        pltpu.make_async_copy(whole.at[:, columns(m)], target.at[:, columns(c)], sem)
+        pltpu.make_async_copy(whole.at[:, columns((m + halves) % COLS)], target.at[:, columns(c)], sem)
         for c, m in enumerate(MIRROR)
     ]
 
@@ -210,56 +241,108 @@
             pltpu.make_async_copy(result.at[b], out.at[slots[b]], out_sem.at[b]).wait()
 
 
-def ask_kernel(blocks, where, near, far, *rest):
+def ask_kernel(blocks, where, lefts, *rest):
     n = len(blocks)
+    left_refs, rest = rest[:lefts], rest[lefts:]
     refs, rest = rest[: n_arrays(where)], rest[n_arrays(where) :]
     outs, (left, right, left_sem, sem) = rest[:-4], rest[-4:]
-    core, j, v = place(*blocks[0])
-    alike = all(t == 1 for t, _ in blocks)
-    if alike:
-        use_near = jnp.where(core == 0, v > j, v < j)
-
-        @pl.when(use_near)
-        def _():
-            for copy in load_mirrored(near, left.at[0], left_sem):
-                copy.start()
-
-        @pl.when(jnp.logical_not(use_near))
-        def _():
-            for copy in load_mirrored(far, left.at[0], left_sem):
-                copy.start()
+    core, _, x, _ = where_am_i()
+    plane = (lax.rem(lax.div(lax.axis_index("row"), 2), 2) == 0) != (core == 0)
+
+    def body():
+        left_copies = load_mirrored(left_refs[0], left.at[0], left_sem, 4 if lefts == 1 else 0)
+        copies = [load([(refs[i], p) for i, p in where[b]], right.at[b], sem.at[b]) for b in range(n)]
+        for copy in left_copies + [c for row in copies for c in row]:
+            copy.start()
+        if lefts > 1:
+            for wanted, ref in ((plane, left_refs[1]), (jnp.logical_not(plane), left_refs[2])):
+                @pl.when(wanted)
+                def _():
+                    for copy in load_mirrored(ref, left.at[1], left_sem):
+                        copy.start()
+
+            left_copies += load_mirrored(left_refs[1], left.at[1], left_sem)
+        for copy in left_copies:
+            copy.wait()
+        for b in range(n):
+            for copy in copies[b]:
+                copy.wait()
+            if lefts == 1:
+                multiply(left.at[0], right.at[b], outs[0].at[b])
+            else:
+                _, j, v = place(*blocks[b])
+                chosen = jnp.where(jnp.where(core == 0, v > j, v < j), 0, 1)
+                multiply(left.at[chosen], right.at[b], outs[b])
+
+    if lefts == 1:
+        pl.when((core == 0) == (x == 0))(body)
     else:
-        for copy in load_mirrored(near, left.at[0], left_sem) + load_mirrored(far, left.at[1], left_sem):
+        body()
+
+
+def both_kernel(blocks, where, neighbours, counts, weights, near, *rest):
+    n = len(blocks)
+    refs, (_, out, answers, left, right, result, left_sem, sem, out_sem) = rest[:-9], rest[-9:]
+    core, j, x, _ = where_am_i()
+    asks = (core == 0) == (x == 0)
+    slots = [slot_for(neighbours, counts, place(t, r)[2] - j) for t, r in blocks]
+    copies = [load([(refs[i], p) for i, p in where[b]], right.at[b], sem.at[b]) for b in range(n)]
+
+    @pl.when(asks)
+    def _():
+        for copy in load_mirrored(near, left.at[0], left_sem.at[0]):
             copy.start()
+
+    for copy in [c for row in copies for c in row]:
+        copy.start()
+    pltpu.make_async_copy(weights, left.at[1], left_sem.at[1]).start()
+
+    @pl.when(asks)
+    def _():
+        for copy in load_mirrored(near, left.at[0], left_sem.at[0]):
+            copy.wait()
+
     for b in range(n):
-        for copy in load([(refs[i], p) for i, p in where[b]], right.at[b], sem.at[b]):
-            copy.start()
-    for copy in load_mirrored(near, left.at[0], left_sem):
-        copy.wait()
-    if not alike:
-        for copy in load_mirrored(far, left.at[1], left_sem):
+        for copy in copies[b]:
             copy.wait()
+
+        @pl.when(asks)
+        def _():
+            multiply(left.at[0], right.at[b], answers.at[b])
+
+    pltpu.make_async_copy(weights, left.at[1], left_sem.at[1]).wait()
     for b in range(n):
-        for copy in load([(refs[i], p) for i, p in where[b]], right.at[b], sem.at[b]):
-            copy.wait()
-        _, _, v = place(*blocks[b])
-        chosen = 0 if alike else jnp.where(jnp.where(core == 0, v > j, v < j), 0, 1)
-        multiply(left.at[chosen], right.at[b], outs[0].at[b] if alike else outs[b])
+        @pl.when(slots[b] < NNB)
+        def _():
+            multiply(left.at[1], right.at[b], result.at[b])
+            pltpu.make_async_copy(result.at[b], out.at[slots[b]], out_sem.at[b]).start()
+    for b in range(n):
+        @pl.when(slots[b] < NNB)
+        def _():
+            pltpu.make_async_copy(result.at[b], out.at[slots[b]], out_sem.at[b]).wait()
 
 
 def gather_kernel(steps, where, neighbours, counts, *rest):
     n = len(steps)
     refs, (_, out, held, sem, out_sem) = rest[:-5], rest[-5:]
     sources = [refs[i] if p is None else refs[i].at[p] for i, p in where]
+    core, _, x, _ = where_am_i()
+    from_across = (core == 0) == (x == 0)
+    slots = []
+    for i, (t, r, kind) in enumerate(steps):
+        slot = result_slot(neighbours, counts, t, r, True)
+        if kind:
+            slot = jnp.where(from_across if kind == "across" else jnp.logical_not(from_across), slot, NNB)
+        slots.append(slot)
+
+        @pl.when(slot < NNB)
+        def _():
+            pltpu.make_async_copy(sources[i], held.at[i], sem.at[i]).start()
+
     for i in range(n):
-        pltpu.make_async_copy(sources[i], held.at[i], sem.at[i]).start()
-    slots = []
-    for i, (t, r) in enumerate(steps):
-        slots.append(result_slot(neighbours, counts, t, r, True))
-        pltpu.make_async_copy(sources[i], held.at[i], sem.at[i]).wait()
-
         @pl.when(slots[i] < NNB)
         def _():
+            pltpu.make_async_copy(sources[i], held.at[i], sem.at[i]).wait()
             pltpu.make_async_copy(held.at[i], out.at[slots[i]], out_sem.at[i]).start()
 
     for i in range(n):
@@ -345,24 +428,44 @@
     )(neighbours, counts, weights, *arrays, *extra)
 
 
-def ask_products(blocks, near, far, parts):
+def ask_products(blocks, lefts, parts):
     arrays, where = distinct(parts)
-    n = len(blocks)
-    alike = all(t == 1 for t, _ in blocks)
+    m, n = len(lefts), len(blocks)
     return pl.pallas_call(
-        functools.partial(ask_kernel, blocks, where),
-        out_shape=jax.ShapeDtypeStruct((n, BS, BS), jnp.bfloat16) if alike else [RESULT] * n,
-        in_specs=[ANY] * (2 + len(arrays)),
-        out_specs=VMEM if alike else [VMEM] * n,
+        functools.partial(ask_kernel, blocks, where, m),
+        out_shape=jax.ShapeDtypeStruct((n, BS, BS), jnp.bfloat16) if m == 1 else [RESULT] * n,
+        in_specs=[ANY] * (m + len(arrays)),
+        out_specs=VMEM if m == 1 else [VMEM] * n,
         scratch_shapes=[
-            pltpu.VMEM((1 if alike else 2, BS, STATES), jnp.bfloat16),
+            pltpu.VMEM((min(m, 2), BS, STATES), jnp.bfloat16),
             pltpu.VMEM((n, BS, STATES), jnp.bfloat16),
             pltpu.SemaphoreType.DMA, pltpu.SemaphoreType.DMA((n,)),
         ],
         cost_estimate=cost(n),
         compiler_params=limit(20),
         name="ask_products",
-    )(near, far, *arrays)
+    )(*lefts, *arrays)
+
+
+def both_products(blocks, neighbours, counts, weights, near, parts, out):
+    arrays, where = distinct(parts)
+    m, n = len(arrays), len(blocks)
+    return pl.pallas_call(
+        functools.partial(both_kernel, blocks, where),
+        out_shape=[OUT, jax.ShapeDtypeStruct((n, BS, BS), jnp.bfloat16)],
+        in_specs=[SMEM, SMEM] + [ANY] * (3 + m),
+        out_specs=[ANY, VMEM],
+        scratch_shapes=[
+            pltpu.VMEM((2, BS, STATES), jnp.bfloat16),
+            pltpu.VMEM((n, BS, STATES), jnp.bfloat16),
+            pltpu.VMEM((n, BS, BS), jnp.bfloat16),
+            pltpu.SemaphoreType.DMA((2,)), pltpu.SemaphoreType.DMA((n,)), pltpu.SemaphoreType.DMA((n,)),
+        ],
+        input_output_aliases={4 + m: 0},
+        cost_estimate=cost(2 * n),
+        compiler_params=limit(20),
+        name="both_products",
+    )(neighbours, counts, weights, near, *arrays, out)
 
 
 def gather(steps, neighbours, counts, results, out):
@@ -378,7 +481,7 @@
             pltpu.SemaphoreType.DMA((n,)), pltpu.SemaphoreType.DMA((n,)),
         ],
         input_output_aliases={2 + len(arrays): 0},
-        compiler_params=limit(8),
+        compiler_params=limit(10),
         name="place_results",
     )(neighbours, counts, *arrays, out)
 
@@ -393,9 +496,8 @@
     for key in [(x, t, part) for t in range(2) for x in "OP" for part in "AY"]:
         up[key] = send(held[key], move_route(0, 1))
         down[key] = send(held[key], move_route(0, -1))
-        if key[1:] == (1, "Y"):
-            other = far_up["P" if key[0] == "O" else "O", 0, "Y"]
-            far_up[key] = send(other, move_route(1, 0))
+        if key == ("O", 1, "Y"):
+            far_up[key] = send(far_up["P", 0, "Y"], move_route(1, 0))
         else:
             far_up[key] = send(up[key], move_route(0, 1))
 
@@ -411,23 +513,31 @@
 
     weights = weigh(occupations.reshape(COLS, KS), parts_of(0, 0))
     near = send(weights, swap_route())
-    far = send(weights, edge_route())
+    far_in = send(weights, edge_route())
+    along_y, along_x = plane_routes()
+    far_out = send(send(weights, along_y), along_x)
+    across = send(weights, across_route())
     out = own_products(((0, 0),), neighbours, counts, weights, [parts_of(0, 0)], None)
 
-    half = ((0, 3), (0, 1), (0, 2))
-    parts = [parts_of(*b) for b in half]
-    out = own_products(half, neighbours, counts, weights, parts, out)
-    answers = ask_products(half, near, far, parts)
-    back = [(send(a, result_route(*b)), None) for a, b in zip(answers, half)]
-    early, late = ((1, 0), (1, 1)), ((1, 3), (1, 2))
-    for pair in (early, late):
+    rest = ((0, 3), (0, 1), (0, 2))
+    parts = [parts_of(*b) for b in rest]
+    out = own_products(rest, neighbours, counts, weights, parts, out)
+    answers = ask_products(rest, [near, far_in, far_out], parts)
+    back = [(send(a, result_route(b[1])), None) for a, b in zip(answers, rest)]
+    steps = [(0, r, None) for _, r in rest]
+    whole = ((0, 3), (0, 0), (0, 1), (0, 2))
+    answer = ask_products(whole, [across], [parts_of(*b) for b in whole])
+    answer = send(answer, across_route())
+    back += [(answer, i) for i in range(4)]
+    steps += [(1, r, "across") for _, r in whole]
+    for pair in (((1, 0), (1, 3)), ((1, 1), (1, 2))):
         parts = [parts_of(*b) for b in pair]
-        answer = ask_products(pair, near, far, parts)
-        answer = send(answer, result_route(*pair[0]))
+        out, answer = both_products(pair, neighbours, counts, weights, near, parts, out)
+        answer = send(answer, near_route())
         back += [(answer, 0), (answer, 1)]
-        out = own_products(pair, neighbours, counts, weights, parts, out)
-    out = gather(half + early, neighbours, counts, back[:5], out)
-    out = gather(late, neighbours, counts, back[5:], out)
+        steps += [(1, r, "near") for _, r in pair]
+    out = gather(tuple(steps[:7]), neighbours, counts, back[:7], out)
+    out = gather(tuple(steps[7:]), neighbours, counts, back[7:], out)
     return out[None]
 
 

time: 205 us -> 239 us (1.17)
  the two profiles are of different devices: /device:TPU:9 before, /device:TPU:8 now
where the time goes in v1:
time: 239 us
  waiting for transfers between devices  119 us (50%)
  starting transfers between devices  65.3 us (27%)
  Pallas kernels  45.1 us (19%)
  local copies, waits for them, and re-layouts  7.58 us (3%)
    ppermute x39, waiting for transfers between devices, send(): return lax.ppermute(value, AXES, route)  119 us
    ppermute x39, starting transfers between devices, send(): return lax.ppermute(value, AXES, route)  65.3 us
    pallas_call x2, Pallas kernels, both_products(): pl.pallas_call(functools.partial(both_kernel, blocks, where), out_shape=[...  16.6 us
    pallas_call x2, Pallas kernels, ask_products(): pl.pallas_call(functools.partial(ask_kernel, blocks, where, m), out_shape...  13.6 us
    pallas_call x2, Pallas kernels, own_products(): pl.pallas_call(functools.partial(own_kernel, blocks, first, where), out_s...  9.59 us
    unnamed x44, local copies, waits for them, and re-layouts  7.58 us
  transfers between devices with their start and end apart: 39, of which 16 were waited for; matrix products, arithmetic and copies ran while one was open for 0% of the time, Pallas kernels for 18%

profile of v1, /device:TPU:8, one launch (start us, length us, event | category | flops | bytes accessed | tf_op | source)
XLA Modules:
  0.0 238.6 jit_solution(3200794027501764640)
XLA Ops:
  0.0 1.6 copy-done.14
  1.6 0.7 copy-done.20
  2.2 1.8 pick.1
  4.0 3.1 %collective-permute-start.4 = (bf16[2,512,256]{2,1,0:T(8,128)(2,1)}, bf16[2,512,256]{2,1,0:T(8,128)(2,1)S(1)}, u32[]{:S(2)}, u32[]{:S(2)}) collective-permute-start(bf16[2,512,256]{2,1,0:T(8,128)(2,1)} %get-tuple-element.19.rest_0_), channel_id=1, source_target_pairs={{4,0},{5,1},{6,2},{7,3},{0,4},{1,5},{2,6},{3,7},{12,8},{13,9},{14,... | collective-permute-start | bytes 1572872 | tf_op jit(solution)/shard_map/ppermute | solution.py:105
  7.1 1.9 collective-permute-start
  9.0 0.5 collective-permute-start.3
  9.5 2.1 collective-permute-start.2
  11.7 8.9 %collective-permute-done.4.rest_12_.rest_15_ = bf16[2,512,256]{2,1,0:T(8,128)(2,1)S(1)} collective-permute-done((bf16[2,512,256]{2,1,0:T(8,128)(2,1)}, bf16[2,512,256]{2,1,0:T(8,128)(2,1)S(1)}, u32[]{:S(2)}, u32[]{:S(2)}) %collective-permute-start.4) | collective-permute-done | bytes 524320 | tf_op jit(solution)/shard_map/ppermute | solution.py:105
  20.6 4.0 %collective-permute-start.22 = (bf16[2,512,256]{2,1,0:T(8,128)(2,1)S(1)}, bf16[2,512,256]{2,1,0:T(8,128)(2,1)S(1)}, u32[]{:S(2)}, u32[]{:S(2)}) collective-permute-start(bf16[2,512,256]{2,1,0:T(8,128)(2,1)S(1)} %get-tuple-element.17.rest_8_.rest_11_.rest_13_), channel_id=1, source_target_pairs={{1,0},{2,1},{3,2},{0,3},{5,4},{6,5},{7,6},{4,7},{11,8},{8,9},{9,10... | collective-permute-start | bytes 1572872 | tf_op jit(solution)/shard_map/ppermute | solution.py:105
  24.7 6.1 %collective-permute-done.3.rest_4_.rest_7_.rest_5_ = bf16[2,512,256]{2,1,0:T(8,128)(2,1)S(1)} collective-permute-done((bf16[2,512,256]{2,1,0:T(8,128)(2,1)}, bf16[2,512,256]{2,1,0:T(8,128)(2,1)S(1)}, u32[]{:S(2)}, u32[]{:S(2)}) %collective-permute-start.3) | collective-permute-done | bytes 524320 | tf_op jit(solution)/shard_map/ppermute | solution.py:105
  30.7 3.0 %collective-permute-start.12 = (bf16[2,512,256]{2,1,0:T(8,128)(2,1)S(1)}, bf16[2,512,256]{2,1,0:T(8,128)(2,1)S(1)}, u32[]{:S(2)}, u32[]{:S(2)}) collective-permute-start(bf16[2,512,256]{2,1,0:T(8,128)(2,1)S(1)} %get-tuple-element.16.rest_0_.rest_3_.rest_1_), channel_id=1, source_target_pairs={{4,0},{5,1},{6,2},{7,3},{0,4},{1,5},{2,6},{3,7},{12,8},{13,9},{14,... | collective-permute-start | bytes 1572872 | tf_op jit(solution)/shard_map/ppermute | solution.py:105
  33.7 0.5 collective-permute-start.13
  34.3 0.8 copy-done.6
  35.1 1.9 collective-permute-start.1
  37.0 0.8 copy-done.12
  37.8 3.7 %collective-permute-start.7 = (bf16[2,512,256]{2,1,0:T(8,128)(2,1)S(1)}, bf16[2,512,256]{2,1,0:T(8,128)(2,1)S(1)}, u32[]{:S(2)}, u32[]{:S(2)}) collective-permute-start(bf16[2,512,256]{2,1,0:T(8,128)(2,1)S(1)} %collective-permute-done.3.rest_4_.rest_7_.rest_5_), channel_id=1, source_target_pairs={{1,0},{2,1},{3,2},{0,3},{5,4},{6,5},{7,6},{4,7},{11,8},{8,9},{9,10... | collective-permute-start | bytes 1572872 | tf_op jit(solution)/shard_map/ppermute | solution.py:105
  41.5 5.6 %collective-permute-done.12.rest_4_ = bf16[2,512,256]{2,1,0:T(8,128)(2,1)S(1)} collective-permute-done((bf16[2,512,256]{2,1,0:T(8,128)(2,1)S(1)}, bf16[2,512,256]{2,1,0:T(8,128)(2,1)S(1)}, u32[]{:S(2)}, u32[]{:S(2)}) %collective-permute-start.12) | collective-permute-done | bytes 524320 | tf_op jit(solution)/shard_map/ppermute | solution.py:105
  47.0 1.9 collective-permute-start.9
  48.9 7.3 %collective-permute-done.13.rest_4_ = bf16[2,512,256]{2,1,0:T(8,128)(2,1)S(1)} collective-permute-done((bf16[2,512,256]{2,1,0:T(8,128)(2,1)S(1)}, bf16[2,512,256]{2,1,0:T(8,128)(2,1)S(1)}, u32[]{:S(2)}, u32[]{:S(2)}) %collective-permute-start.13) | collective-permute-done | bytes 524320 | tf_op jit(solution)/shard_map/ppermute | solution.py:105
  56.3 4.0 %collective-permute-start.11 = (bf16[2,512,256]{2,1,0:T(8,128)(2,1)}, bf16[2,512,256]{2,1,0:T(8,128)(2,1)}, u32[]{:S(2)}, u32[]{:S(2)}) collective-permute-start(bf16[2,512,256]{2,1,0:T(8,128)(2,1)} %get-tuple-element.18.rest_0_), channel_id=1, source_target_pairs={{1,0},{2,1},{3,2},{0,3},{5,4},{6,5},{7,6},{4,7},{11,8},{8,9},{9,10... | collective-permute-start | bytes 1572872 | tf_op jit(solution)/shard_map/ppermute | solution.py:105
  60.3 0.8 copy-done
  61.1 3.2 %collective-permute-start.18 = (bf16[2,512,256]{2,1,0:T(8,128)(2,1)}, bf16[2,512,256]{2,1,0:T(8,128)(2,1)}, u32[]{:S(2)}, u32[]{:S(2)}) collective-permute-start(bf16[2,512,256]{2,1,0:T(8,128)(2,1)} %get-tuple-element.19.rest_0_), channel_id=1, source_target_pairs={{1,0},{2,1},{3,2},{0,3},{5,4},{6,5},{7,6},{4,7},{11,8},{8,9},{9,10... | collective-permute-start | bytes 1572872 | tf_op jit(solution)/shard_map/ppermute | solution.py:105
  64.4 0.0 copy-start.3
  64.4 0.8 copy-done.3
  65.2 1.0 copy-done.1
  66.2 1.0 copy-done.4
  67.3 0.8 weigh.1.weights
  68.1 2.5 %collective-permute-start.32 = (bf16[512,2048]{1,0:T(8,128)(2,1)S(1)}, bf16[512,2048]{1,0:T(8,128)(2,1)S(1)}, u32[]{:S(2)}, u32[]{:S(2)}) collective-permute-start(bf16[512,2048]{1,0:T(8,128)(2,1)S(1)} %weigh.1.weights), channel_id=1, source_target_pairs={{24,56},{25,57},{26,58},{27,59},{28,60},{29,61},{30,62},{31,63},{3... | collective-permute-start | bytes 6291464 | tf_op jit(solution)/shard_map/ppermute | solution.py:105
  70.6 2.3 collective-permute-done.11.rest_3_
  72.9 2.2 collective-permute-start.37
  75.1 3.3 %collective-permute-done.17.rest_8_ = bf16[2,512,256]{2,1,0:T(8,128)(2,1)} collective-permute-done((bf16[2,512,256]{2,1,0:T(8,128)(2,1)}, bf16[2,512,256]{2,1,0:T(8,128)(2,1)}, u32[]{:S(2)}, u32[]{:S(2)}) %collective-permute-start.17) | collective-permute-done | bytes 524320 | tf_op jit(solution)/shard_map/ppermute | solution.py:105
  78.4 0.2 collective-permute-start.25
  78.6 5.6 %collective-permute-done.18.rest_9_ = bf16[2,512,256]{2,1,0:T(8,128)(2,1)} collective-permute-done((bf16[2,512,256]{2,1,0:T(8,128)(2,1)}, bf16[2,512,256]{2,1,0:T(8,128)(2,1)}, u32[]{:S(2)}, u32[]{:S(2)}) %collective-permute-start.18) | collective-permute-done | bytes 524320 | tf_op jit(solution)/shard_map/ppermute | solution.py:105
  84.2 3.7 %collective-permute-start.24 = (bf16[2,512,256]{2,1,0:T(8,128)(2,1)S(1)}, bf16[2,512,256]{2,1,0:T(8,128)(2,1)S(1)}, u32[]{:S(2)}, u32[]{:S(2)}) collective-permute-start(bf16[2,512,256]{2,1,0:T(8,128)(2,1)S(1)} %copy-done.9), channel_id=1, source_target_pairs={{1,0},{2,1},{3,2},{0,3},{5,4},{6,5},{7,6},{4,7},{11,8},{8,9},{9,10... | collective-permute-start | bytes 1572872 | tf_op jit(solution)/shard_map/ppermute | solution.py:105
  87.9 8.8 %collective-permute-done.25.rest_10_.rest_13_.rest_14_ = bf16[2,512,256]{2,1,0:T(8,128)(2,1)S(1)} collective-permute-done((bf16[2,512,256]{2,1,0:T(8,128)(2,1)S(1)}, bf16[2,512,256]{2,1,0:T(8,128)(2,1)S(1)}, u32[]{:S(2)}, u32[]{:S(2)}) %collective-permute-start.25) | collective-permute-done | bytes 524320 | tf_op jit(solution)/shard_map/ppermute | solution.py:105
  96.7 3.5 %collective-permute-done.24.rest_7_.rest_10_.rest_8_ = bf16[2,512,256]{2,1,0:T(8,128)(2,1)S(1)} collective-permute-done((bf16[2,512,256]{2,1,0:T(8,128)(2,1)S(1)}, bf16[2,512,256]{2,1,0:T(8,128)(2,1)S(1)}, u32[]{:S(2)}, u32[]{:S(2)}) %collective-permute-start.24) | collective-permute-done | bytes 524320 | tf_op jit(solution)/shard_map/ppermute | solution.py:105
  100.2 3.7 %collective-permute-start.16 = (bf16[2,512,256]{2,1,0:T(8,128)(2,1)S(1)}, bf16[2,512,256]{2,1,0:T(8,128)(2,1)S(1)}, u32[]{:S(2)}, u32[]{:S(2)}) collective-permute-start(bf16[2,512,256]{2,1,0:T(8,128)(2,1)S(1)} %copy-done.18), channel_id=1, source_target_pairs={{1,0},{2,1},{3,2},{0,3},{5,4},{6,5},{7,6},{4,7},{11,8},{8,9},{9,10... | collective-permute-start | bytes 1572872 | tf_op jit(solution)/shard_map/ppermute | solution.py:105
  103.9 0.2 collective-permute-done.19.rest_10_
  104.0 0.7 collective-permute-start.14
  104.8 11.1 %collective-permute-done.16.rest_7_ = bf16[2,512,256]{2,1,0:T(8,128)(2,1)S(1)} collective-permute-done((bf16[2,512,256]{2,1,0:T(8,128)(2,1)S(1)}, bf16[2,512,256]{2,1,0:T(8,128)(2,1)S(1)}, u32[]{:S(2)}, u32[]{:S(2)}) %collective-permute-start.16) | collective-permute-done | bytes 524320 | tf_op jit(solution)/shard_map/ppermute | solution.py:105
  115.9 3.7 %collective-permute-start.20 = (bf16[2,512,256]{2,1,0:T(8,128)(2,1)S(1)}, bf16[2,512,256]{2,1,0:T(8,128)(2,1)S(1)}, u32[]{:S(2)}, u32[]{:S(2)}) collective-permute-start(bf16[2,512,256]{2,1,0:T(8,128)(2,1)S(1)} %copy-done.16), channel_id=1, source_target_pairs={{1,0},{2,1},{3,2},{0,3},{5,4},{6,5},{7,6},{4,7},{11,8},{8,9},{9,10... | collective-permute-start | bytes 1572872 | tf_op jit(solution)/shard_map/ppermute | solution.py:105
  119.6 12.3 %collective-permute-done.20.rest_11_ = bf16[2,512,256]{2,1,0:T(8,128)(2,1)S(1)} collective-permute-done((bf16[2,512,256]{2,1,0:T(8,128)(2,1)S(1)}, bf16[2,512,256]{2,1,0:T(8,128)(2,1)S(1)}, u32[]{:S(2)}, u32[]{:S(2)}) %collective-permute-start.20) | collective-permute-done | bytes 524320 | tf_op jit(solution)/shard_map/ppermute | solution.py:105
  131.9 1.9 collective-permute-start.15
  133.8 0.8 collective-permute-start.31
  134.6 2.1 collective-permute-start.33
  136.7 7.5 %ask_products.3 = bf16[4,512,512]{2,1,0:T(8,128)(2,1)S(1)} custom-call(bf16[512,2048]{1,0:T(8,128)(2,1)S(1)} %collective-permute-done.37.rest_0_, bf16[2,512,256]{2,1,0:T(8,128)(2,1)S(1)} %get-tuple-element.16.rest_0_.rest_3_.rest_1_, bf16[2,512,256]{2,1,0:T(8,128)(2,1)S(1)} %copy-done.11, ...), custom_call_target="tpu_custom_call" | custom-call | flops 4294967296 | bytes 9437184 | tf_op jit(solution)/shard_map/ask_products/pallas_call | solution.py:434
  144.2 1.9 collective-permute-start.38
  146.8 5.4 %own_products.2.rest_16_ = bf16[15,512,512]{2,1,0:T(8,128)(2,1)} custom-call(s32[1,15]{1,0:T(1,128)S(1)} %copy-done.19, s32[1]{0:T(128)S(6)} %copy.16.counts, bf16[512,2048]{1,0:T(8,128)(2,1)S(1)} %weigh.1.weights, bf16[2,512,256]{2,1,0:T(8,128)(2,1)S(1)} %get-tuple-element.16.rest_0_.rest_3_.rest_1_, ...), custom_call_target="tpu_custom_call" | custom-call | flops 1073741824 | bytes 2359296 | tf_op jit(solution)/shard_map/own_products/pallas_call | solution.py:415
  152.2 3.5 %collective-permute-start.29 = (bf16[2,512,256]{2,1,0:T(8,128)(2,1)S(1)}, bf16[2,512,256]{2,1,0:T(8,128)(2,1)S(1)}, u32[]{:S(2)}, u32[]{:S(2)}) collective-permute-start(bf16[2,512,256]{2,1,0:T(8,128)(2,1)S(1)} %collective-permute-done.19.rest_10_), channel_id=1, source_target_pairs={{3,0},{0,1},{1,2},{2,3},{7,4},{4,5},{5,6},{6,7},{9,8},{10,9},{11,1... | collective-permute-start | bytes 1572872 | tf_op jit(solution)/shard_map/ppermute | solution.py:105
  155.7 4.2 %own_products.3.rest_12_ = bf16[15,512,512]{2,1,0:T(8,128)(2,1)} custom-call(s32[1,15]{1,0:T(1,128)S(1)} %copy-done.19, s32[1]{0:T(128)S(6)} %copy.16.counts, bf16[512,2048]{1,0:T(8,128)(2,1)S(1)} %weigh.1.weights, bf16[2,512,256]{2,1,0:T(8,128)(2,1)S(1)} %get-tuple-element.16.rest_0_.rest_3_.rest_1_, ...), custom_call_target="tpu_custom_call", output_to_operand_aliasing={{}: (19, {})} | custom-call | flops 3221225472 | bytes 7077888 | tf_op jit(solution)/shard_map/own_products/pallas_call | solution.py:415
  159.9 7.5 %both_products.2 = (bf16[15,512,512]{2,1,0:T(8,128)(2,1)}, bf16[2,512,512]{2,1,0:T(8,128)(2,1)S(1)}) custom-call(s32[1,15]{1,0:T(1,128)S(1)} %copy-done.19, s32[1]{0:T(128)S(6)} %copy.16.counts, bf16[512,2048]{1,0:T(8,128)(2,1)S(1)} %weigh.1.weights, bf16[512,2048]{1,0:T(8,128)(2,1)S(1)} %collective-permute-done.8.near.rest_0_, ...), custom_call_target="tpu_custom_call", output_to_operand_aliasing={{0}: (16, {})} | custom-call | flops 4294967296 | bytes 9437184 | tf_op jit(solution)/shard_map/both_products/pallas_call | solution.py:453
  167.4 27.6 %collective-permute-done.28.rest_2_ = bf16[2,512,256]{2,1,0:T(8,128)(2,1)S(1)} collective-permute-done((bf16[2,512,256]{2,1,0:T(8,128)(2,1)S(1)}, bf16[2,512,256]{2,1,0:T(8,128)(2,1)S(1)}, u32[]{:S(2)}, u32[]{:S(2)}) %collective-permute-start.28) | collective-permute-done | bytes 524320 | tf_op jit(solution)/shard_map/ppermute | solution.py:105
  195.0 9.2 %both_products.3 = (bf16[15,512,512]{2,1,0:T(8,128)(2,1)}, bf16[2,512,512]{2,1,0:T(8,128)(2,1)S(1)}) custom-call(s32[1,15]{1,0:T(1,128)S(1)} %copy-done.19, s32[1]{0:T(128)S(6)} %copy.16.counts, bf16[512,2048]{1,0:T(8,128)(2,1)S(1)} %weigh.1.weights, bf16[512,2048]{1,0:T(8,128)(2,1)S(1)} %collective-permute-done.8.near.rest_0_, ...), custom_call_target="tpu_custom_call", output_to_operand_aliasing={{0}: (16, {})} | custom-call | flops 4294967296 | bytes 9437184 | tf_op jit(solution)/shard_map/both_products/pallas_call | solution.py:453
  204.1 1.4 collective-permute-start.30
  205.5 1.4 collective-permute-start.27
  206.9 6.1 %ask_products.2 = (bf16[512,512]{1,0:T(8,128)(2,1)S(1)}, bf16[512,512]{1,0:T(8,128)(2,1)S(1)}, bf16[512,512]{1,0:T(8,128)(2,1)S(1)}) custom-call(bf16[512,2048]{1,0:T(8,128)(2,1)S(1)} %collective-permute-done.8.near.rest_0_, bf16[512,2048]{1,0:T(8,128)(2,1)S(1)} %collective-permute-done.31.rest_1_, bf16[512,2048]{1,0:T(8,128)(2,1)S(1)} %collective-permute-done.33.rest_2_, ...), custom_call_target="tpu_custom_call" | custom-call | flops 3221225472 | bytes 7077888 | tf_op jit(solution)/shard_map/ask_products/pallas_call | solution.py:434
  213.0 1.9 collective-permute-start.34
  214.9 1.9 collective-permute-start.35
  216.9 1.9 collective-permute-start.36
  218.8 5.6 %collective-permute-done.34.rest_0_ = bf16[512,512]{1,0:T(8,128)(2,1)S(1)} collective-permute-done((bf16[512,512]{1,0:T(8,128)(2,1)S(1)}, bf16[512,512]{1,0:T(8,128)(2,1)S(1)}, u32[]{:S(2)}, u32[]{:S(2)}) %collective-permute-start.34) | collective-permute-done | bytes 524320 | tf_op jit(solution)/shard_map/ppermute | solution.py:105
  224.4 5.6 %collective-permute-done.35.rest_1_ = bf16[512,512]{1,0:T(8,128)(2,1)S(1)} collective-permute-done((bf16[512,512]{1,0:T(8,128)(2,1)S(1)}, bf16[512,512]{1,0:T(8,128)(2,1)S(1)}, u32[]{:S(2)}, u32[]{:S(2)}) %collective-permute-start.35) | collective-permute-done | bytes 524320 | tf_op jit(solution)/shard_map/ppermute | solution.py:105
  230.0 5.6 %collective-permute-done.36.rest_2_ = bf16[512,512]{1,0:T(8,128)(2,1)S(1)} collective-permute-done((bf16[512,512]{1,0:T(8,128)(2,1)S(1)}, bf16[512,512]{1,0:T(8,128)(2,1)S(1)}, u32[]{:S(2)}, u32[]{:S(2)}) %collective-permute-start.36) | collective-permute-done | bytes 524320 | tf_op jit(solution)/shard_map/ppermute | solution.py:105
  235.7 2.0 place_results.2.rest_2_
  237.6 0.8 place_results.3
  (69 shorter events, 0.2 us)
Async XLA Ops:
  0.0 1.6 copy-start.14
  1.6 0.7 copy-start.20
  2.2 62.9 %copy-start.21 = (f32[2048]{0:T(1024)S(1)}, f32[2048]{0:T(1024)}, u32[]{:S(2)}) copy-start(f32[2048]{0:T(1024)} %param.6) | copy-start | bytes 24580
  4.0 16.6 %collective-permute-start.4 = (bf16[2,512,256]{2,1,0:T(8,128)(2,1)}, bf16[2,512,256]{2,1,0:T(8,128)(2,1)S(1)}, u32[]{:S(2)}, u32[]{:S(2)}) collective-permute-start(bf16[2,512,256]{2,1,0:T(8,128)(2,1)} %get-tuple-element.19.rest_0_), channel_id=1, source_target_pairs={{4,0},{5,1},{6,2},{7,3},{0,4},{1,5},{2,6},{3,7},{12,8},{13,9},{14,... | collective-permute-start | bytes 1572872 | tf_op jit(solution)/shard_map/ppermute | solution.py:105
  7.1 17.5 %collective-permute-start = (bf16[2,512,256]{2,1,0:T(8,128)(2,1)S(1)}, bf16[2,512,256]{2,1,0:T(8,128)(2,1)S(1)}, u32[]{:S(2)}, u32[]{:S(2)}) collective-permute-start(bf16[2,512,256]{2,1,0:T(8,128)(2,1)S(1)} %get-tuple-element.17.rest_8_.rest_11_.rest_13_), channel_id=1, source_target_pairs={{3,0},{0,1},{1,2},{2,3},{7,4},{4,5},{5,6},{6,7},{9,8},{10,9},{11,1... | collective-permute-start | bytes 1572872 | tf_op jit(solution)/shard_map/ppermute | solution.py:105
  9.0 21.7 %collective-permute-start.3 = (bf16[2,512,256]{2,1,0:T(8,128)(2,1)}, bf16[2,512,256]{2,1,0:T(8,128)(2,1)S(1)}, u32[]{:S(2)}, u32[]{:S(2)}) collective-permute-start(bf16[2,512,256]{2,1,0:T(8,128)(2,1)} %get-tuple-element.18.rest_0_), channel_id=1, source_target_pairs={{4,0},{5,1},{6,2},{7,3},{0,4},{1,5},{2,6},{3,7},{12,8},{13,9},{14,... | collective-permute-start | bytes 1572872 | tf_op jit(solution)/shard_map/ppermute | solution.py:105
  9.5 24.2 %collective-permute-start.2 = (bf16[2,512,256]{2,1,0:T(8,128)(2,1)S(1)}, bf16[2,512,256]{2,1,0:T(8,128)(2,1)S(1)}, u32[]{:S(2)}, u32[]{:S(2)}) collective-permute-start(bf16[2,512,256]{2,1,0:T(8,128)(2,1)S(1)} %get-tuple-element.16.rest_0_.rest_3_.rest_1_), channel_id=1, source_target_pairs={{1,0},{2,1},{3,2},{0,3},{5,4},{6,5},{7,6},{4,7},{11,8},{8,9},{9,10... | collective-permute-start | bytes 1572872 | tf_op jit(solution)/shard_map/ppermute | solution.py:105
  11.7 23.4 %collective-permute-start.21 = (bf16[2,512,256]{2,1,0:T(8,128)(2,1)S(1)}, bf16[2,512,256]{2,1,0:T(8,128)(2,1)S(1)}, u32[]{:S(2)}, u32[]{:S(2)}) collective-permute-start(bf16[2,512,256]{2,1,0:T(8,128)(2,1)S(1)} %get-tuple-element.16.rest_0_.rest_3_.rest_1_), channel_id=1, source_target_pairs={{3,0},{0,1},{1,2},{2,3},{7,4},{4,5},{5,6},{6,7},{9,8},{10,9},{11,1... | collective-permute-start | bytes 1572872 | tf_op jit(solution)/shard_map/ppermute | solution.py:105
  20.6 20.8 %copy-start.8 = (bf16[2,512,256]{2,1,0:T(8,128)(2,1)}, bf16[2,512,256]{2,1,0:T(8,128)(2,1)S(1)}, u32[]{:S(2)}) copy-start(bf16[2,512,256]{2,1,0:T(8,128)(2,1)S(1)} %collective-permute-done.4.rest_12_.rest_15_) | copy-start | bytes 1572868
  20.6 16.4 %collective-permute-start.22 = (bf16[2,512,256]{2,1,0:T(8,128)(2,1)S(1)}, bf16[2,512,256]{2,1,0:T(8,128)(2,1)S(1)}, u32[]{:S(2)}, u32[]{:S(2)}) collective-permute-start(bf16[2,512,256]{2,1,0:T(8,128)(2,1)S(1)} %get-tuple-element.17.rest_8_.rest_11_.rest_13_), channel_id=1, source_target_pairs={{1,0},{2,1},{3,2},{0,3},{5,4},{6,5},{7,6},{4,7},{11,8},{8,9},{9,10... | collective-permute-start | bytes 1572872 | tf_op jit(solution)/shard_map/ppermute | solution.py:105
  24.7 16.8 %collective-permute-start.5 = (bf16[2,512,256]{2,1,0:T(8,128)(2,1)S(1)}, bf16[2,512,256]{2,1,0:T(8,128)(2,1)S(1)}, u32[]{:S(2)}, u32[]{:S(2)}) collective-permute-start(bf16[2,512,256]{2,1,0:T(8,128)(2,1)S(1)} %collective-permute-done.4.rest_12_.rest_15_), channel_id=1, source_target_pairs={{3,0},{0,1},{1,2},{2,3},{7,4},{4,5},{5,6},{6,7},{9,8},{10,9},{11,1... | collective-permute-start | bytes 1572872 | tf_op jit(solution)/shard_map/ppermute | solution.py:105
  30.7 16.3 %collective-permute-start.12 = (bf16[2,512,256]{2,1,0:T(8,128)(2,1)S(1)}, bf16[2,512,256]{2,1,0:T(8,128)(2,1)S(1)}, u32[]{:S(2)}, u32[]{:S(2)}) collective-permute-start(bf16[2,512,256]{2,1,0:T(8,128)(2,1)S(1)} %get-tuple-element.16.rest_0_.rest_3_.rest_1_), channel_id=1, source_target_pairs={{4,0},{5,1},{6,2},{7,3},{0,4},{1,5},{2,6},{3,7},{12,8},{13,9},{14,... | collective-permute-start | bytes 1572872 | tf_op jit(solution)/shard_map/ppermute | solution.py:105
  33.7 22.5 %collective-permute-start.13 = (bf16[2,512,256]{2,1,0:T(8,128)(2,1)S(1)}, bf16[2,512,256]{2,1,0:T(8,128)(2,1)S(1)}, u32[]{:S(2)}, u32[]{:S(2)}) collective-permute-start(bf16[2,512,256]{2,1,0:T(8,128)(2,1)S(1)} %get-tuple-element.17.rest_8_.rest_11_.rest_13_), channel_id=1, source_target_pairs={{4,0},{5,1},{6,2},{7,3},{0,4},{1,5},{2,6},{3,7},{12,8},{13,9},{14,... | collective-permute-start | bytes 1572872 | tf_op jit(solution)/shard_map/ppermute | solution.py:105
  34.2 0.8 copy-start.6
  35.1 1.9 copy-start.10
  35.1 25.2 %collective-permute-start.1 = (bf16[2,512,256]{2,1,0:T(8,128)(2,1)S(1)}, bf16[2,512,256]{2,1,0:T(8,128)(2,1)S(1)}, u32[]{:S(2)}, u32[]{:S(2)}) collective-permute-start(bf16[2,512,256]{2,1,0:T(8,128)(2,1)S(1)} %collective-permute-done.rest_1_.rest_9_.rest_12_), channel_id=1, source_target_pairs={{3,0},{0,1},{1,2},{2,3},{7,4},{4,5},{5,6},{6,7},{9,8},{10,9},{11,1... | collective-permute-start | bytes 1572872 | tf_op jit(solution)/shard_map/ppermute | solution.py:105
  37.0 0.8 copy-start.12
  37.8 22.5 %collective-permute-start.7 = (bf16[2,512,256]{2,1,0:T(8,128)(2,1)S(1)}, bf16[2,512,256]{2,1,0:T(8,128)(2,1)S(1)}, u32[]{:S(2)}, u32[]{:S(2)}) collective-permute-start(bf16[2,512,256]{2,1,0:T(8,128)(2,1)S(1)} %collective-permute-done.3.rest_4_.rest_7_.rest_5_), channel_id=1, source_target_pairs={{1,0},{2,1},{3,2},{0,3},{5,4},{6,5},{7,6},{4,7},{11,8},{8,9},{9,10... | collective-permute-start | bytes 1572872 | tf_op jit(solution)/shard_map/ppermute | solution.py:105
  41.5 22.9 %collective-permute-start.6 = (bf16[2,512,256]{2,1,0:T(8,128)(2,1)S(1)}, bf16[2,512,256]{2,1,0:T(8,128)(2,1)S(1)}, u32[]{:S(2)}, u32[]{:S(2)}) collective-permute-start(bf16[2,512,256]{2,1,0:T(8,128)(2,1)S(1)} %collective-permute-done.5.rest_5_.rest_13_.rest_16_.rest_11_), channel_id=1, source_target_pairs={{3,0},{0,1},{1,2},{2,3},{7,4},{4,5},{5,6},{6,7},{9,8},{10,9},{11,1... | collective-permute-start | bytes 1572872 | tf_op jit(solution)/shard_map/ppermute | solution.py:105
  47.0 17.4 %copy-start.17 = (bf16[2,512,256]{2,1,0:T(8,128)(2,1)}, bf16[2,512,256]{2,1,0:T(8,128)(2,1)S(1)}, u32[]{:S(2)}) copy-start(bf16[2,512,256]{2,1,0:T(8,128)(2,1)S(1)} %collective-permute-done.12.rest_4_) | copy-start | bytes 1572868
  47.0 21.1 %collective-permute-start.9 = (bf16[2,512,256]{2,1,0:T(8,128)(2,1)}, bf16[2,512,256]{2,1,0:T(8,128)(2,1)}, u32[]{:S(2)}, u32[]{:S(2)}) collective-permute-start(bf16[2,512,256]{2,1,0:T(8,128)(2,1)} %get-tuple-element.19.rest_0_), channel_id=1, source_target_pairs={{3,0},{0,1},{1,2},{2,3},{7,4},{4,5},{5,6},{6,7},{9,8},{10,9},{11,1... | collective-permute-start | bytes 1572872 | tf_op jit(solution)/shard_map/ppermute | solution.py:105
  56.3 8.1 %copy-start.15 = (bf16[2,512,256]{2,1,0:T(8,128)(2,1)}, bf16[2,512,256]{2,1,0:T(8,128)(2,1)S(1)}, u32[]{:S(2)}) copy-start(bf16[2,512,256]{2,1,0:T(8,128)(2,1)S(1)} %collective-permute-done.13.rest_4_) | copy-start | bytes 1572868
  56.3 16.7 %collective-permute-start.11 = (bf16[2,512,256]{2,1,0:T(8,128)(2,1)}, bf16[2,512,256]{2,1,0:T(8,128)(2,1)}, u32[]{:S(2)}, u32[]{:S(2)}) collective-permute-start(bf16[2,512,256]{2,1,0:T(8,128)(2,1)} %get-tuple-element.18.rest_0_), channel_id=1, source_target_pairs={{1,0},{2,1},{3,2},{0,3},{5,4},{6,5},{7,6},{4,7},{11,8},{8,9},{9,10... | collective-permute-start | bytes 1572872 | tf_op jit(solution)/shard_map/ppermute | solution.py:105
  60.3 18.1 %collective-permute-start.17 = (bf16[2,512,256]{2,1,0:T(8,128)(2,1)}, bf16[2,512,256]{2,1,0:T(8,128)(2,1)}, u32[]{:S(2)}, u32[]{:S(2)}) collective-permute-start(bf16[2,512,256]{2,1,0:T(8,128)(2,1)} %get-tuple-element.18.rest_0_), channel_id=1, source_target_pairs={{3,0},{0,1},{1,2},{2,3},{7,4},{4,5},{5,6},{6,7},{9,8},{10,9},{11,1... | collective-permute-start | bytes 1572872 | tf_op jit(solution)/shard_map/ppermute | solution.py:105
  60.3 0.8 copy-start
  61.1 23.0 %collective-permute-start.18 = (bf16[2,512,256]{2,1,0:T(8,128)(2,1)}, bf16[2,512,256]{2,1,0:T(8,128)(2,1)}, u32[]{:S(2)}, u32[]{:S(2)}) collective-permute-start(bf16[2,512,256]{2,1,0:T(8,128)(2,1)} %get-tuple-element.19.rest_0_), channel_id=1, source_target_pairs={{1,0},{2,1},{3,2},{0,3},{5,4},{6,5},{7,6},{4,7},{11,8},{8,9},{9,10... | collective-permute-start | bytes 1572872 | tf_op jit(solution)/shard_map/ppermute | solution.py:105
  64.4 0.8 copy-start.3
  65.2 22.7 %collective-permute-start.23 = (bf16[2,512,256]{2,1,0:T(8,128)(2,1)S(1)}, bf16[2,512,256]{2,1,0:T(8,128)(2,1)}, u32[]{:S(2)}, u32[]{:S(2)}) collective-permute-start(bf16[2,512,256]{2,1,0:T(8,128)(2,1)S(1)} %collective-permute-done.3.rest_4_.rest_7_.rest_5_), channel_id=1, source_target_pairs={{3,0},{0,1},{1,2},{2,3},{7,4},{4,5},{5,6},{6,7},{9,8},{10,9},{11,1... | collective-permute-start | bytes 1572872 | tf_op jit(solution)/shard_map/ppermute | solution.py:105
  65.2 1.0 copy-start.1
  66.2 1.0 copy-start.4
  67.3 11.1 %copy-start.11 = (bf16[2,512,256]{2,1,0:T(8,128)(2,1)S(1)}, bf16[2,512,256]{2,1,0:T(8,128)(2,1)}, u32[]{:S(2)}) copy-start(bf16[2,512,256]{2,1,0:T(8,128)(2,1)} %copy-done.10) | copy-start | bytes 1572868
  67.3 16.9 %copy-start.9 = (bf16[2,512,256]{2,1,0:T(8,128)(2,1)S(1)}, bf16[2,512,256]{2,1,0:T(8,128)(2,1)}, u32[]{:S(2)}) copy-start(bf16[2,512,256]{2,1,0:T(8,128)(2,1)} %copy-done.8) | copy-start | bytes 1572868
  67.3 20.6 %copy-start.18 = (bf16[2,512,256]{2,1,0:T(8,128)(2,1)S(1)}, bf16[2,512,256]{2,1,0:T(8,128)(2,1)}, u32[]{:S(2)}) copy-start(bf16[2,512,256]{2,1,0:T(8,128)(2,1)} %copy-done.17) | copy-start | bytes 1572868
  67.3 36.7 %copy-start.16 = (bf16[2,512,256]{2,1,0:T(8,128)(2,1)S(1)}, bf16[2,512,256]{2,1,0:T(8,128)(2,1)}, u32[]{:S(2)}) copy-start(bf16[2,512,256]{2,1,0:T(8,128)(2,1)} %copy-done.15) | copy-start | bytes 1572868
  67.3 69.4 %copy-start.2 = (bf16[2,512,256]{2,1,0:T(8,128)(2,1)S(1)}, bf16[2,512,256]{2,1,0:T(8,128)(2,1)}, u32[]{:S(2)}) copy-start(bf16[2,512,256]{2,1,0:T(8,128)(2,1)} %copy-done) | copy-start | bytes 1572868
  67.3 69.4 %copy-start.5 = (bf16[2,512,256]{2,1,0:T(8,128)(2,1)S(1)}, bf16[2,512,256]{2,1,0:T(8,128)(2,1)}, u32[]{:S(2)}) copy-start(bf16[2,512,256]{2,1,0:T(8,128)(2,1)} %copy-done.3) | copy-start | bytes 1572868
  67.3 69.4 %copy-start.7 = (bf16[2,512,256]{2,1,0:T(8,128)(2,1)S(1)}, bf16[2,512,256]{2,1,0:T(8,128)(2,1)}, u32[]{:S(2)}) copy-start(bf16[2,512,256]{2,1,0:T(8,128)(2,1)} %copy-done.6) | copy-start | bytes 1572868
  67.3 69.4 %copy-start.13 = (bf16[2,512,256]{2,1,0:T(8,128)(2,1)S(1)}, bf16[2,512,256]{2,1,0:T(8,128)(2,1)}, u32[]{:S(2)}) copy-start(bf16[2,512,256]{2,1,0:T(8,128)(2,1)} %copy-done.12) | copy-start | bytes 1572868
  68.1 78.7 %copy-start.19 = (s32[1,15]{1,0:T(1,128)S(1)}, s32[1,15]{1,0:T(1,128)}, u32[]{:S(2)}) copy-start(s32[1,15]{1,0:T(1,128)} %neighbours.11) | copy-start | bytes 184
  68.1 65.6 %collective-permute-start.32 = (bf16[512,2048]{1,0:T(8,128)(2,1)S(1)}, bf16[512,2048]{1,0:T(8,128)(2,1)S(1)}, u32[]{:S(2)}, u32[]{:S(2)}) collective-permute-start(bf16[512,2048]{1,0:T(8,128)(2,1)S(1)} %weigh.1.weights), channel_id=1, source_target_pairs={{24,56},{25,57},{26,58},{27,59},{28,60},{29,61},{30,62},{31,63},{3... | collective-permute-start | bytes 6291464 | tf_op jit(solution)/shard_map/ppermute | solution.py:105
  72.9 61.6 %collective-permute-start.37 = (bf16[512,2048]{1,0:T(8,128)(2,1)S(1)}, bf16[512,2048]{1,0:T(8,128)(2,1)S(1)}, u32[]{:S(2)}, u32[]{:S(2)}) collective-permute-start(bf16[512,2048]{1,0:T(8,128)(2,1)S(1)} %weigh.1.weights), channel_id=1, source_target_pairs={{12,16},{13,17},{14,18},{15,19},{16,12},{17,13},{18,14},{19,15},{2... | collective-permute-start | bytes 6291464 | tf_op jit(solution)/shard_map/ppermute | solution.py:105
  78.4 18.3 %collective-permute-start.25 = (bf16[2,512,256]{2,1,0:T(8,128)(2,1)S(1)}, bf16[2,512,256]{2,1,0:T(8,128)(2,1)S(1)}, u32[]{:S(2)}, u32[]{:S(2)}) collective-permute-start(bf16[2,512,256]{2,1,0:T(8,128)(2,1)S(1)} %copy-done.11), channel_id=1, source_target_pairs={{3,0},{0,1},{1,2},{2,3},{7,4},{4,5},{5,6},{6,7},{9,8},{10,9},{11,1... | collective-permute-start | bytes 1572872 | tf_op jit(solution)/shard_map/ppermute | solution.py:105
  84.2 16.0 %collective-permute-start.24 = (bf16[2,512,256]{2,1,0:T(8,128)(2,1)S(1)}, bf16[2,512,256]{2,1,0:T(8,128)(2,1)S(1)}, u32[]{:S(2)}, u32[]{:S(2)}) collective-permute-start(bf16[2,512,256]{2,1,0:T(8,128)(2,1)S(1)} %copy-done.9), channel_id=1, source_target_pairs={{1,0},{2,1},{3,2},{0,3},{5,4},{6,5},{7,6},{4,7},{11,8},{8,9},{9,10... | collective-permute-start | bytes 1572872 | tf_op jit(solution)/shard_map/ppermute | solution.py:105
  87.9 16.2 %collective-permute-start.19 = (bf16[2,512,256]{2,1,0:T(8,128)(2,1)S(1)}, bf16[2,512,256]{2,1,0:T(8,128)(2,1)S(1)}, u32[]{:S(2)}, u32[]{:S(2)}) collective-permute-start(bf16[2,512,256]{2,1,0:T(8,128)(2,1)S(1)} %copy-done.18), channel_id=1, source_target_pairs={{3,0},{0,1},{1,2},{2,3},{7,4},{4,5},{5,6},{6,7},{9,8},{10,9},{11,1... | collective-permute-start | bytes 1572872 | tf_op jit(solution)/shard_map/ppermute | solution.py:105
  96.7 59.0 %collective-permute-start.8 = (bf16[512,2048]{1,0:T(8,128)(2,1)S(1)}, bf16[512,2048]{1,0:T(8,128)(2,1)S(1)}, u32[]{:S(2)}, u32[]{:S(2)}) collective-permute-start(bf16[512,2048]{1,0:T(8,128)(2,1)S(1)} %weigh.1.weights), channel_id=1, source_target_pairs={{0,8},{1,9},{2,10},{3,11},{4,12},{5,13},{6,14},{7,15},{8,0},{9,1},... | collective-permute-start | bytes 6291464 | tf_op jit(solution)/shard_map/ppermute | solution.py:105
  100.2 15.7 %collective-permute-start.16 = (bf16[2,512,256]{2,1,0:T(8,128)(2,1)S(1)}, bf16[2,512,256]{2,1,0:T(8,128)(2,1)S(1)}, u32[]{:S(2)}, u32[]{:S(2)}) collective-permute-start(bf16[2,512,256]{2,1,0:T(8,128)(2,1)S(1)} %copy-done.18), channel_id=1, source_target_pairs={{1,0},{2,1},{3,2},{0,3},{5,4},{6,5},{7,6},{4,7},{11,8},{8,9},{9,10... | collective-permute-start | bytes 1572872 | tf_op jit(solution)/shard_map/ppermute | solution.py:105
  104.0 15.5 %collective-permute-start.14 = (bf16[2,512,256]{2,1,0:T(8,128)(2,1)S(1)}, bf16[2,512,256]{2,1,0:T(8,128)(2,1)S(1)}, u32[]{:S(2)}, u32[]{:S(2)}) collective-permute-start(bf16[2,512,256]{2,1,0:T(8,128)(2,1)S(1)} %copy-done.16), channel_id=1, source_target_pairs={{3,0},{0,1},{1,2},{2,3},{7,4},{4,5},{5,6},{6,7},{9,8},{10,9},{11,1... | collective-permute-start | bytes 1572872 | tf_op jit(solution)/shard_map/ppermute | solution.py:105
  115.9 16.0 %collective-permute-start.20 = (bf16[2,512,256]{2,1,0:T(8,128)(2,1)S(1)}, bf16[2,512,256]{2,1,0:T(8,128)(2,1)S(1)}, u32[]{:S(2)}, u32[]{:S(2)}) collective-permute-start(bf16[2,512,256]{2,1,0:T(8,128)(2,1)S(1)} %copy-done.16), channel_id=1, source_target_pairs={{1,0},{2,1},{3,2},{0,3},{5,4},{6,5},{7,6},{4,7},{11,8},{8,9},{9,10... | collective-permute-start | bytes 1572872 | tf_op jit(solution)/shard_map/ppermute | solution.py:105
  119.6 12.3 %collective-permute-start.26 = (bf16[2,512,256]{2,1,0:T(8,128)(2,1)}, bf16[2,512,256]{2,1,0:T(8,128)(2,1)S(1)}, u32[]{:S(2)}, u32[]{:S(2)}) collective-permute-start(bf16[2,512,256]{2,1,0:T(8,128)(2,1)} %collective-permute-done.23.rest_5_.rest_8_.rest_6_), channel_id=1, source_target_pairs={{3,0},{0,1},{1,2},{2,3},{7,4},{4,5},{5,6},{6,7},{9,8},{10,9},{11,1... | collective-permute-start | bytes 1572872 | tf_op jit(solution)/shard_map/ppermute | solution.py:105
  131.9 12.3 %collective-permute-start.10 = (bf16[2,512,256]{2,1,0:T(8,128)(2,1)}, bf16[2,512,256]{2,1,0:T(8,128)(2,1)S(1)}, u32[]{:S(2)}, u32[]{:S(2)}) collective-permute-start(bf16[2,512,256]{2,1,0:T(8,128)(2,1)} %collective-permute-done.9.rest_1_), channel_id=1, source_target_pairs={{3,0},{0,1},{1,2},{2,3},{7,4},{4,5},{5,6},{6,7},{9,8},{10,9},{11,1... | collective-permute-start | bytes 1572872 | tf_op jit(solution)/shard_map/ppermute | solution.py:105
  131.9 20.3 %collective-permute-start.15 = (bf16[2,512,256]{2,1,0:T(8,128)(2,1)S(1)}, bf16[2,512,256]{2,1,0:T(8,128)(2,1)S(1)}, u32[]{:S(2)}, u32[]{:S(2)}) collective-permute-start(bf16[2,512,256]{2,1,0:T(8,128)(2,1)S(1)} %collective-permute-done.14.rest_5_), channel_id=1, source_target_pairs={{3,0},{0,1},{1,2},{2,3},{7,4},{4,5},{5,6},{6,7},{9,8},{10,9},{11,1... | collective-permute-start | bytes 1572872 | tf_op jit(solution)/shard_map/ppermute | solution.py:105
  133.8 73.1 %collective-permute-start.31 = (bf16[512,2048]{1,0:T(8,128)(2,1)S(1)}, bf16[512,2048]{1,0:T(8,128)(2,1)S(1)}, u32[]{:S(2)}, u32[]{:S(2)}) collective-permute-start(bf16[512,2048]{1,0:T(8,128)(2,1)S(1)} %weigh.1.weights), channel_id=1, source_target_pairs={{8,16},{9,17},{10,18},{11,19},{12,20},{13,21},{14,22},{15,23},{16,... | collective-permute-start | bytes 6291464 | tf_op jit(solution)/shard_map/ppermute | solution.py:105
  134.6 72.3 %collective-permute-start.33 = (bf16[512,2048]{1,0:T(8,128)(2,1)S(1)}, bf16[512,2048]{1,0:T(8,128)(2,1)S(1)}, u32[]{:S(2)}, u32[]{:S(2)}) collective-permute-start(bf16[512,2048]{1,0:T(8,128)(2,1)S(1)} %collective-permute-done.32), channel_id=1, source_target_pairs={{56,32},{57,33},{58,34},{59,35},{60,36},{61,37},{62,38},{63,39},{0... | collective-permute-start | bytes 6291464 | tf_op jit(solution)/shard_map/ppermute | solution.py:105
  144.2 72.7 %collective-permute-start.38 = (bf16[4,512,512]{2,1,0:T(8,128)(2,1)S(1)}, bf16[4,512,512]{2,1,0:T(8,128)(2,1)S(1)}, u32[]{:S(2)}, u32[]{:S(2)}) collective-permute-start(bf16[4,512,512]{2,1,0:T(8,128)(2,1)S(1)} %ask_products.3), channel_id=1, source_target_pairs={{12,16},{13,17},{14,18},{15,19},{16,12},{17,13},{18,14},{19,15},{2... | collective-permute-start | bytes 6291464 | tf_op jit(solution)/shard_map/ppermute | solution.py:105
  152.2 15.2 %collective-permute-start.29 = (bf16[2,512,256]{2,1,0:T(8,128)(2,1)S(1)}, bf16[2,512,256]{2,1,0:T(8,128)(2,1)S(1)}, u32[]{:S(2)}, u32[]{:S(2)}) collective-permute-start(bf16[2,512,256]{2,1,0:T(8,128)(2,1)S(1)} %collective-permute-done.19.rest_10_), channel_id=1, source_target_pairs={{3,0},{0,1},{1,2},{2,3},{7,4},{4,5},{5,6},{6,7},{9,8},{10,9},{11,1... | collective-permute-start | bytes 1572872 | tf_op jit(solution)/shard_map/ppermute | solution.py:105
  155.7 39.3 %collective-permute-start.28 = (bf16[2,512,256]{2,1,0:T(8,128)(2,1)S(1)}, bf16[2,512,256]{2,1,0:T(8,128)(2,1)S(1)}, u32[]{:S(2)}, u32[]{:S(2)}) collective-permute-start(bf16[2,512,256]{2,1,0:T(8,128)(2,1)S(1)} %collective-permute-done.26.rest_14_.rest_17_.rest_16_), channel_id=1, source_target_pairs={{4,0},{5,1},{6,2},{7,3},{0,4},{1,5},{2,6},{3,7},{12,8},{13,9},{14,... | collective-permute-start | bytes 1572872 | tf_op jit(solution)/shard_map/ppermute | solution.py:105
  204.1 33.5 %collective-permute-start.30 = (bf16[2,512,512]{2,1,0:T(8,128)(2,1)S(1)}, bf16[2,512,512]{2,1,0:T(8,128)(2,1)S(1)}, u32[]{:S(2)}, u32[]{:S(2)}) collective-permute-start(bf16[2,512,512]{2,1,0:T(8,128)(2,1)S(1)} %get-tuple-element.22), channel_id=1, source_target_pairs={{0,8},{1,9},{2,10},{3,11},{12,4},{13,5},{14,6},{15,7},{16,24},{17,... | collective-permute-start | bytes 3145736 | tf_op jit(solution)/shard_map/ppermute | solution.py:105
  205.5 32.1 %collective-permute-start.27 = (bf16[2,512,512]{2,1,0:T(8,128)(2,1)S(1)}, bf16[2,512,512]{2,1,0:T(8,128)(2,1)S(1)}, u32[]{:S(2)}, u32[]{:S(2)}) collective-permute-start(bf16[2,512,512]{2,1,0:T(8,128)(2,1)S(1)} %get-tuple-element.20), channel_id=1, source_target_pairs={{0,8},{1,9},{2,10},{3,11},{12,4},{13,5},{14,6},{15,7},{16,24},{17,... | collective-permute-start | bytes 3145736 | tf_op jit(solution)/shard_map/ppermute | solution.py:105
  213.0 11.4 %collective-permute-start.34 = (bf16[512,512]{1,0:T(8,128)(2,1)S(1)}, bf16[512,512]{1,0:T(8,128)(2,1)S(1)}, u32[]{:S(2)}, u32[]{:S(2)}) collective-permute-start(bf16[512,512]{1,0:T(8,128)(2,1)S(1)} %get-tuple-element.23), channel_id=1, source_target_pairs={{0,8},{4,12},{8,16},{9,17},{10,18},{11,3},{12,20},{13,21},{14,22},... | collective-permute-start | bytes 1572872 | tf_op jit(solution)/shard_map/ppermute | solution.py:105
  214.9 15.1 %collective-permute-start.35 = (bf16[512,512]{1,0:T(8,128)(2,1)S(1)}, bf16[512,512]{1,0:T(8,128)(2,1)S(1)}, u32[]{:S(2)}, u32[]{:S(2)}) collective-permute-start(bf16[512,512]{1,0:T(8,128)(2,1)S(1)} %get-tuple-element.24), channel_id=1, source_target_pairs={{0,8},{1,9},{2,10},{4,12},{5,13},{6,14},{8,16},{9,1},{10,2},{11,3}... | collective-permute-start | bytes 1572872 | tf_op jit(solution)/shard_map/ppermute | solution.py:105
  216.9 18.8 %collective-permute-start.36 = (bf16[512,512]{1,0:T(8,128)(2,1)S(1)}, bf16[512,512]{1,0:T(8,128)(2,1)S(1)}, u32[]{:S(2)}, u32[]{:S(2)}) collective-permute-start(bf16[512,512]{1,0:T(8,128)(2,1)S(1)} %get-tuple-element.25), channel_id=1, source_target_pairs={{0,8},{1,9},{4,12},{5,13},{8,16},{9,17},{10,2},{11,3},{12,20},{13,... | collective-permute-start | bytes 1572872 | tf_op jit(solution)/shard_map/ppermute | solution.py:105

commit v2 on v1

--- a/solution.py
+++ b/solution.py
@@ -82,6 +82,21 @@
         if 0 <= to < 8 and asks_near(c, x):
             pairs.append((index(k, c, x, z), index(to, tc, 1 - x, z)))
     return pairs
+
+
+def answer_routes():
+    direct, first, second = [], [], []
+    for k, c, x, z in devices():
+        to, tc = partner_of(k, c)
+        if 0 <= to < 8 and asks_near(c, x):
+            here, there = index(k, c, x, z), index(to, tc, 1 - x, z)
+            if in_plane(k, c):
+                direct.append((here, there))
+            else:
+                middle = index(2 * to - k, c, x, z)
+                first.append((here, middle))
+                second.append((middle, there))
+    return direct, first, second
 
 
 def near_route():
@@ -328,11 +343,17 @@
     sources = [refs[i] if p is None else refs[i].at[p] for i, p in where]
     core, _, x, _ = where_am_i()
     from_across = (core == 0) == (x == 0)
+    plane = (lax.rem(lax.div(lax.axis_index("row"), 2), 2) == 0) != (core == 0)
+    when = {
+        "near": jnp.logical_not(from_across),
+        "across": from_across & plane,
+        "planes": from_across & jnp.logical_not(plane),
+    }
     slots = []
     for i, (t, r, kind) in enumerate(steps):
         slot = result_slot(neighbours, counts, t, r, True)
         if kind:
-            slot = jnp.where(from_across if kind == "across" else jnp.logical_not(from_across), slot, NNB)
+            slot = jnp.where(when[kind], slot, NNB)
         slots.append(slot)
 
         @pl.when(slot < NNB)
@@ -527,17 +548,19 @@
     steps = [(0, r, None) for _, r in rest]
     whole = ((0, 3), (0, 0), (0, 1), (0, 2))
     answer = ask_products(whole, [across], [parts_of(*b) for b in whole])
-    answer = send(answer, across_route())
-    back += [(answer, i) for i in range(4)]
-    steps += [(1, r, "across") for _, r in whole]
+    direct, along_y, along_x = answer_routes()
+    first = send(answer, along_y)
+    for kind, got in (("across", send(answer, direct)), ("planes", send(first, along_x))):
+        back += [(got, i) for i in range(4)]
+        steps += [(1, r, kind) for _, r in whole]
     for pair in (((1, 0), (1, 3)), ((1, 1), (1, 2))):
         parts = [parts_of(*b) for b in pair]
         out, answer = both_products(pair, neighbours, counts, weights, near, parts, out)
         answer = send(answer, near_route())
         back += [(answer, 0), (answer, 1)]
         steps += [(1, r, "near") for _, r in pair]
-    out = gather(tuple(steps[:7]), neighbours, counts, back[:7], out)
-    out = gather(tuple(steps[7:]), neighbours, counts, back[7:], out)
+    out = gather(tuple(steps[:11]), neighbours, counts, back[:11], out)
+    out = gather(tuple(steps[11:]), neighbours, counts, back[11:], out)
     return out[None]
 
 

time: 239 us -> 235 us (0.983)
  the two profiles are of different devices: /device:TPU:8 before, /device:TPU:119 now
where the time goes in v2:
time: 235 us; the launch traced here: 234 us
  waiting for transfers between devices  128 us (54%)
  starting transfers between devices  54.3 us (23%)
  Pallas kernels  48.9 us (21%)
    ppermute x41, waiting for transfers between devices, send(): return lax.ppermute(value, AXES, route)  128 us
    ppermute x41, starting transfers between devices, send(): return lax.ppermute(value, AXES, route)  54.3 us
    pallas_call x2, Pallas kernels, both_products(): pl.pallas_call(functools.partial(both_kernel, blocks, where), out_shape=[...  17.3 us
    pallas_call x2, Pallas kernels, ask_products(): pl.pallas_call(functools.partial(ask_kernel, blocks, where, m), out_shape...  13.6 us
    pallas_call x2, Pallas kernels, own_products(): pl.pallas_call(functools.partial(own_kernel, blocks, first, where), out_s...  11.6 us
  transfers between devices with their start and end apart: 41, of which 22 were waited for; matrix products, arithmetic and copies ran while one was open for 0% of the time, Pallas kernels for 20%

profile of v2, /device:TPU:119, one launch (start us, length us, event | category | flops | bytes accessed | tf_op | source)
XLA Modules:
  0.0 234.3 jit_solution(3844904369045093924)
XLA Ops:
  0.0 1.6 copy-done.4
  1.6 0.7 copy-done.10
  2.2 0.7 pick.1
  3.0 1.2 collective-permute-start.4
  4.4 1.8 collective-permute-start.3
  6.2 11.2 %collective-permute-done.4.rest_12_.rest_15_ = bf16[2,512,256]{2,1,0:T(8,128)(2,1)S(1)} collective-permute-done((bf16[2,512,256]{2,1,0:T(8,128)(2,1)S(1)}, bf16[2,512,256]{2,1,0:T(8,128)(2,1)S(1)}, u32[]{:S(2)}, u32[]{:S(2)}) %collective-permute-start.4) | collective-permute-done | bytes 524320 | tf_op jit(solution)/shard_map/ppermute | solution.py:120
  17.4 0.1 collective-permute-start.5
  17.5 2.6 %collective-permute-start.2 = (bf16[2,512,256]{2,1,0:T(8,128)(2,1)S(1)}, bf16[2,512,256]{2,1,0:T(8,128)(2,1)S(1)}, u32[]{:S(2)}, u32[]{:S(2)}) collective-permute-start(bf16[2,512,256]{2,1,0:T(8,128)(2,1)S(1)} %get-tuple-element.16.rest_0_.rest_3_.rest_1_), channel_id=1, source_target_pairs={{1,0},{2,1},{3,2},{0,3},{5,4},{6,5},{7,6},{4,7},{11,8},{8,9},{9,10... | collective-permute-start | bytes 1572872 | tf_op jit(solution)/shard_map/ppermute | solution.py:120
  20.1 8.5 %collective-permute-done.3.rest_4_.rest_7_.rest_5_ = bf16[2,512,256]{2,1,0:T(8,128)(2,1)S(1)} collective-permute-done((bf16[2,512,256]{2,1,0:T(8,128)(2,1)S(1)}, bf16[2,512,256]{2,1,0:T(8,128)(2,1)S(1)}, u32[]{:S(2)}, u32[]{:S(2)}) %collective-permute-start.3) | collective-permute-done | bytes 524320 | tf_op jit(solution)/shard_map/ppermute | solution.py:120
  28.7 0.8 collective-permute-done.5.rest_5_.rest_13_.rest_16_.rest_11_
  29.4 0.7 collective-permute-start.6
  30.1 0.2 collective-permute-start.21
  30.4 1.3 collective-permute-done.2.rest_3_.rest_11_.rest_14_.rest_10_
  31.7 9.1 %collective-permute-done.1.rest_2_.rest_5_.rest_3_ = bf16[2,512,256]{2,1,0:T(8,128)(2,1)S(1)} collective-permute-done((bf16[2,512,256]{2,1,0:T(8,128)(2,1)S(1)}, bf16[2,512,256]{2,1,0:T(8,128)(2,1)S(1)}, u32[]{:S(2)}, u32[]{:S(2)}) %collective-permute-start.1) | collective-permute-done | bytes 524320 | tf_op jit(solution)/shard_map/ppermute | solution.py:120
  40.8 2.1 collective-permute-done.7.rest_7_.rest_15_.rest_18_.rest_12_
  42.9 6.3 %collective-permute-done.6.rest_6_.rest_9_.rest_7_ = bf16[2,512,256]{2,1,0:T(8,128)(2,1)} collective-permute-done((bf16[2,512,256]{2,1,0:T(8,128)(2,1)S(1)}, bf16[2,512,256]{2,1,0:T(8,128)(2,1)}, u32[]{:S(2)}, u32[]{:S(2)}) %collective-permute-start.6) | collective-permute-done | bytes 524320 | tf_op jit(solution)/shard_map/ppermute | solution.py:120
  49.2 1.7 weigh.1.weights
  51.0 2.6 %collective-permute-start.37 = (bf16[512,2048]{1,0:T(8,128)(2,1)S(1)}, bf16[512,2048]{1,0:T(8,128)(2,1)S(1)}, u32[]{:S(2)}, u32[]{:S(2)}) collective-permute-start(bf16[512,2048]{1,0:T(8,128)(2,1)S(1)} %weigh.1.weights), channel_id=1, source_target_pairs={{12,16},{13,17},{14,18},{15,19},{16,12},{17,13},{18,14},{19,15},{2... | collective-permute-start | bytes 6291464 | tf_op jit(solution)/shard_map/ppermute | solution.py:120
  53.6 3.6 %collective-permute-start.22 = (bf16[2,512,256]{2,1,0:T(8,128)(2,1)S(1)}, bf16[2,512,256]{2,1,0:T(8,128)(2,1)S(1)}, u32[]{:S(2)}, u32[]{:S(2)}) collective-permute-start(bf16[2,512,256]{2,1,0:T(8,128)(2,1)S(1)} %copy-done.1), channel_id=1, source_target_pairs={{1,0},{2,1},{3,2},{0,3},{5,4},{6,5},{7,6},{4,7},{11,8},{8,9},{9,10... | collective-permute-start | bytes 1572872 | tf_op jit(solution)/shard_map/ppermute | solution.py:120
  57.1 3.0 %collective-permute-start.13 = (bf16[2,512,256]{2,1,0:T(8,128)(2,1)S(1)}, bf16[2,512,256]{2,1,0:T(8,128)(2,1)S(1)}, u32[]{:S(2)}, u32[]{:S(2)}) collective-permute-start(bf16[2,512,256]{2,1,0:T(8,128)(2,1)S(1)} %copy-done.1), channel_id=1, source_target_pairs={{4,0},{5,1},{6,2},{7,3},{0,4},{1,5},{2,6},{3,7},{12,8},{13,9},{14,... | collective-permute-start | bytes 1572872 | tf_op jit(solution)/shard_map/ppermute | solution.py:120
  60.1 6.4 %collective-permute-done.22.rest_3_.rest_6_.rest_4_ = bf16[2,512,256]{2,1,0:T(8,128)(2,1)S(1)} collective-permute-done((bf16[2,512,256]{2,1,0:T(8,128)(2,1)S(1)}, bf16[2,512,256]{2,1,0:T(8,128)(2,1)S(1)}, u32[]{:S(2)}, u32[]{:S(2)}) %collective-permute-start.22) | collective-permute-done | bytes 524320 | tf_op jit(solution)/shard_map/ppermute | solution.py:120
  66.5 1.9 collective-permute-start.32
  68.5 4.1 %collective-permute-done.12.rest_4_ = bf16[2,512,256]{2,1,0:T(8,128)(2,1)S(1)} collective-permute-done((bf16[2,512,256]{2,1,0:T(8,128)(2,1)S(1)}, bf16[2,512,256]{2,1,0:T(8,128)(2,1)S(1)}, u32[]{:S(2)}, u32[]{:S(2)}) %collective-permute-start.12) | collective-permute-done | bytes 524320 | tf_op jit(solution)/shard_map/ppermute | solution.py:120
  72.7 6.8 %collective-permute-done.13.rest_4_ = bf16[2,512,256]{2,1,0:T(8,128)(2,1)S(1)} collective-permute-done((bf16[2,512,256]{2,1,0:T(8,128)(2,1)S(1)}, bf16[2,512,256]{2,1,0:T(8,128)(2,1)S(1)}, u32[]{:S(2)}, u32[]{:S(2)}) %collective-permute-start.13) | collective-permute-done | bytes 524320 | tf_op jit(solution)/shard_map/ppermute | solution.py:120
  79.5 1.1 collective-permute-start.17
  80.6 0.1 collective-permute-start.23
  80.8 2.4 %collective-permute-start.25 = (bf16[2,512,256]{2,1,0:T(8,128)(2,1)}, bf16[2,512,256]{2,1,0:T(8,128)(2,1)S(1)}, u32[]{:S(2)}, u32[]{:S(2)}) collective-permute-start(bf16[2,512,256]{2,1,0:T(8,128)(2,1)} %collective-permute-done.21.rest_1_.rest_4_.rest_2_), channel_id=1, source_target_pairs={{3,0},{0,1},{1,2},{2,3},{7,4},{4,5},{5,6},{6,7},{9,8},{10,9},{11,1... | collective-permute-start | bytes 1572872 | tf_op jit(solution)/shard_map/ppermute | solution.py:120
  83.2 5.7 %collective-permute-done.17.rest_8_ = bf16[2,512,256]{2,1,0:T(8,128)(2,1)S(1)} collective-permute-done((bf16[2,512,256]{2,1,0:T(8,128)(2,1)S(1)}, bf16[2,512,256]{2,1,0:T(8,128)(2,1)S(1)}, u32[]{:S(2)}, u32[]{:S(2)}) %collective-permute-start.17) | collective-permute-done | bytes 524320 | tf_op jit(solution)/shard_map/ppermute | solution.py:120
  88.9 1.8 collective-permute-start.24
  90.7 5.4 %collective-permute-done.23.rest_5_.rest_8_.rest_6_ = bf16[2,512,256]{2,1,0:T(8,128)(2,1)S(1)} collective-permute-done((bf16[2,512,256]{2,1,0:T(8,128)(2,1)S(1)}, bf16[2,512,256]{2,1,0:T(8,128)(2,1)S(1)}, u32[]{:S(2)}, u32[]{:S(2)}) %collective-permute-start.23) | collective-permute-done | bytes 524320 | tf_op jit(solution)/shard_map/ppermute | solution.py:120
  96.1 9.6 %collective-permute-done.25.rest_10_.rest_13_.rest_14_ = bf16[2,512,256]{2,1,0:T(8,128)(2,1)S(1)} collective-permute-done((bf16[2,512,256]{2,1,0:T(8,128)(2,1)}, bf16[2,512,256]{2,1,0:T(8,128)(2,1)S(1)}, u32[]{:S(2)}, u32[]{:S(2)}) %collective-permute-start.25) | collective-permute-done | bytes 524320 | tf_op jit(solution)/shard_map/ppermute | solution.py:120
  105.8 1.8 collective-permute-start.18
  107.6 5.4 %collective-permute-done.26.rest_14_.rest_17_.rest_16_ = bf16[2,512,256]{2,1,0:T(8,128)(2,1)S(1)} collective-permute-done((bf16[2,512,256]{2,1,0:T(8,128)(2,1)S(1)}, bf16[2,512,256]{2,1,0:T(8,128)(2,1)S(1)}, u32[]{:S(2)}, u32[]{:S(2)}) %collective-permute-start.26) | collective-permute-done | bytes 524320 | tf_op jit(solution)/shard_map/ppermute | solution.py:120
  113.0 1.2 collective-permute-start.16
  114.2 0.3 collective-permute-start.14
  114.5 7.5 %ask_products.3 = bf16[4,512,512]{2,1,0:T(8,128)(2,1)S(1)} custom-call(bf16[512,2048]{1,0:T(8,128)(2,1)S(1)} %collective-permute-done.37.rest_0_, bf16[2,512,256]{2,1,0:T(8,128)(2,1)S(1)} %get-tuple-element.16.rest_0_.rest_3_.rest_1_, bf16[2,512,256]{2,1,0:T(8,128)(2,1)} %collective-permute-done.21.rest_1_.rest_4_.rest_2_, ...), custom_call_target="tpu_custom_call" | custom-call | flops 4294967296 | bytes 9437184 | tf_op jit(solution)/shard_map/ask_products/pallas_call | solution.py:455
  122.0 0.8 collective-permute-start.31
  122.8 1.5 collective-permute-done.19.rest_10_
  124.2 0.9 collective-permute-start.8
  125.2 5.8 %collective-permute-done.16.rest_7_ = bf16[2,512,256]{2,1,0:T(8,128)(2,1)S(1)} collective-permute-done((bf16[2,512,256]{2,1,0:T(8,128)(2,1)S(1)}, bf16[2,512,256]{2,1,0:T(8,128)(2,1)S(1)}, u32[]{:S(2)}, u32[]{:S(2)}) %collective-permute-start.16) | collective-permute-done | bytes 524320 | tf_op jit(solution)/shard_map/ppermute | solution.py:120
  131.0 1.9 collective-permute-start.39
  132.9 1.0 collective-permute-done.14.rest_5_
  133.9 2.1 collective-permute-start.20
  135.9 1.9 collective-permute-start.33
  137.8 4.4 %collective-permute-done.20.rest_11_ = bf16[2,512,256]{2,1,0:T(8,128)(2,1)S(1)} collective-permute-done((bf16[2,512,256]{2,1,0:T(8,128)(2,1)S(1)}, bf16[2,512,256]{2,1,0:T(8,128)(2,1)S(1)}, u32[]{:S(2)}, u32[]{:S(2)}) %collective-permute-start.20) | collective-permute-done | bytes 524320 | tf_op jit(solution)/shard_map/ppermute | solution.py:120
  142.2 9.5 %collective-permute-done.10.rest_2_ = bf16[2,512,256]{2,1,0:T(8,128)(2,1)S(1)} collective-permute-done((bf16[2,512,256]{2,1,0:T(8,128)(2,1)S(1)}, bf16[2,512,256]{2,1,0:T(8,128)(2,1)S(1)}, u32[]{:S(2)}, u32[]{:S(2)}) %collective-permute-start.10) | collective-permute-done | bytes 524320 | tf_op jit(solution)/shard_map/ppermute | solution.py:120
  151.7 9.2 %collective-permute-done.15.rest_6_ = bf16[2,512,256]{2,1,0:T(8,128)(2,1)S(1)} collective-permute-done((bf16[2,512,256]{2,1,0:T(8,128)(2,1)S(1)}, bf16[2,512,256]{2,1,0:T(8,128)(2,1)S(1)}, u32[]{:S(2)}, u32[]{:S(2)}) %collective-permute-start.15) | collective-permute-done | bytes 524320 | tf_op jit(solution)/shard_map/ppermute | solution.py:120
  161.0 0.8 collective-permute-start.38
  162.4 4.3 %own_products.2.rest_16_ = bf16[15,512,512]{2,1,0:T(8,128)(2,1)} custom-call(s32[1,15]{1,0:T(1,128)S(1)} %copy-done.9, s32[1]{0:T(128)S(6)} %copy.16.counts, bf16[512,2048]{1,0:T(8,128)(2,1)S(1)} %weigh.1.weights, bf16[2,512,256]{2,1,0:T(8,128)(2,1)S(1)} %get-tuple-element.16.rest_0_.rest_3_.rest_1_, ...), custom_call_target="tpu_custom_call" | custom-call | flops 1073741824 | bytes 2359296 | tf_op jit(solution)/shard_map/own_products/pallas_call | solution.py:436
  166.7 7.3 %own_products.3.rest_12_ = bf16[15,512,512]{2,1,0:T(8,128)(2,1)} custom-call(s32[1,15]{1,0:T(1,128)S(1)} %copy-done.9, s32[1]{0:T(128)S(6)} %copy.16.counts, bf16[512,2048]{1,0:T(8,128)(2,1)S(1)} %weigh.1.weights, bf16[2,512,256]{2,1,0:T(8,128)(2,1)S(1)} %get-tuple-element.16.rest_0_.rest_3_.rest_1_, ...), custom_call_target="tpu_custom_call", output_to_operand_aliasing={{}: (19, {})} | custom-call | flops 3221225472 | bytes 7077888 | tf_op jit(solution)/shard_map/own_products/pallas_call | solution.py:436
  174.1 1.0 collective-permute-start.28
  175.1 9.8 %collective-permute-start.40 = (bf16[4,512,512]{2,1,0:T(8,128)(2,1)S(1)}, bf16[4,512,512]{2,1,0:T(8,128)(2,1)S(1)}, u32[]{:S(2)}, u32[]{:S(2)}) collective-permute-start(bf16[4,512,512]{2,1,0:T(8,128)(2,1)S(1)} %collective-permute-done.39), channel_id=1, source_target_pairs={{60,32},{61,33},{62,34},{63,35},{0,28},{1,29},{2,30},{3,31},{92,64... | collective-permute-start | bytes 6291464 | tf_op jit(solution)/shard_map/ppermute | solution.py:120
  185.0 8.8 %both_products.2 = (bf16[15,512,512]{2,1,0:T(8,128)(2,1)}, bf16[2,512,512]{2,1,0:T(8,128)(2,1)S(1)}) custom-call(s32[1,15]{1,0:T(1,128)S(1)} %copy-done.9, s32[1]{0:T(128)S(6)} %copy.16.counts, bf16[512,2048]{1,0:T(8,128)(2,1)S(1)} %weigh.1.weights, bf16[512,2048]{1,0:T(8,128)(2,1)S(1)} %collective-permute-done.8.near.rest_0_, ...), custom_call_target="tpu_custom_call", output_to_operand_aliasing={{0}: (16, {})} | custom-call | flops 4294967296 | bytes 9437184 | tf_op jit(solution)/shard_map/both_products/pallas_call | solution.py:474
  193.8 6.1 %ask_products.2 = (bf16[512,512]{1,0:T(8,128)(2,1)S(1)}, bf16[512,512]{1,0:T(8,128)(2,1)S(1)}, bf16[512,512]{1,0:T(8,128)(2,1)S(1)}) custom-call(bf16[512,2048]{1,0:T(8,128)(2,1)S(1)} %collective-permute-done.8.near.rest_0_, bf16[512,2048]{1,0:T(8,128)(2,1)S(1)} %collective-permute-done.31.rest_1_, bf16[512,2048]{1,0:T(8,128)(2,1)S(1)} %collective-permute-done.33.rest_2_, ...), custom_call_target="tpu_custom_call" | custom-call | flops 3221225472 | bytes 7077888 | tf_op jit(solution)/shard_map/ask_products/pallas_call | solution.py:455
  199.8 1.9 collective-permute-start.34
  201.8 8.6 %both_products.3 = (bf16[15,512,512]{2,1,0:T(8,128)(2,1)}, bf16[2,512,512]{2,1,0:T(8,128)(2,1)S(1)}) custom-call(s32[1,15]{1,0:T(1,128)S(1)} %copy-done.9, s32[1]{0:T(128)S(6)} %copy.16.counts, bf16[512,2048]{1,0:T(8,128)(2,1)S(1)} %weigh.1.weights, bf16[512,2048]{1,0:T(8,128)(2,1)S(1)} %collective-permute-done.8.near.rest_0_, ...), custom_call_target="tpu_custom_call", output_to_operand_aliasing={{0}: (16, {})} | custom-call | flops 4294967296 | bytes 9437184 | tf_op jit(solution)/shard_map/both_products/pallas_call | solution.py:474
  210.4 1.4 collective-permute-start.30
  211.7 1.4 collective-permute-start.27
  213.1 1.9 collective-permute-start.35
  215.0 1.9 collective-permute-start.36
  217.0 7.5 %collective-permute-done.35.rest_1_ = bf16[512,512]{1,0:T(8,128)(2,1)S(1)} collective-permute-done((bf16[512,512]{1,0:T(8,128)(2,1)S(1)}, bf16[512,512]{1,0:T(8,128)(2,1)S(1)}, u32[]{:S(2)}, u32[]{:S(2)}) %collective-permute-start.35) | collective-permute-done | bytes 524320 | tf_op jit(solution)/shard_map/ppermute | solution.py:120
  224.5 5.6 %collective-permute-done.36.rest_2_ = bf16[512,512]{1,0:T(8,128)(2,1)S(1)} collective-permute-done((bf16[512,512]{1,0:T(8,128)(2,1)S(1)}, bf16[512,512]{1,0:T(8,128)(2,1)S(1)}, u32[]{:S(2)}, u32[]{:S(2)}) %collective-permute-start.36) | collective-permute-done | bytes 524320 | tf_op jit(solution)/shard_map/ppermute | solution.py:120
  230.1 3.2 %place_results.2.rest_2_ = bf16[15,512,512]{2,1,0:T(8,128)(2,1)} custom-call(s32[1,15]{1,0:T(1,128)S(1)} %copy-done.9, s32[1]{0:T(128)S(6)} %copy.16.counts, bf16[512,512]{1,0:T(8,128)(2,1)S(1)} %collective-permute-done.34.rest_0_, bf16[512,512]{1,0:T(8,128)(2,1)S(1)} %collective-permute-done.35.rest_1_, ...), custom_call_target="tpu_custom_call", output_to_operand_aliasing={{}: (7, {})} | custom-call | tf_op jit(solution)/shard_map/place_results/pallas_call | solution.py:495
  233.3 0.8 place_results.3
  (53 shorter events, 0.5 us)
Async XLA Ops:
  0.0 1.6 copy-start.4
  1.6 0.7 copy-start.10
  2.2 28.1 %copy-start.11 = (f32[2048]{0:T(1024)S(1)}, f32[2048]{0:T(1024)}, u32[]{:S(2)}) copy-start(f32[2048]{0:T(1024)} %param.6) | copy-start | bytes 24580
  3.0 26.5 %copy-start = (bf16[2,512,256]{2,1,0:T(8,128)(2,1)}, bf16[2,512,256]{2,1,0:T(8,128)(2,1)S(1)}, u32[]{:S(2)}) copy-start(bf16[2,512,256]{2,1,0:T(8,128)(2,1)S(1)} %get-tuple-element.17.rest_8_.rest_11_.rest_13_) | copy-start | bytes 1572868
  3.0 27.1 %copy-start.5 = (bf16[2,512,256]{2,1,0:T(8,128)(2,1)}, bf16[2,512,256]{2,1,0:T(8,128)(2,1)S(1)}, u32[]{:S(2)}) copy-start(bf16[2,512,256]{2,1,0:T(8,128)(2,1)S(1)} %get-tuple-element.19.rest_0_) | copy-start | bytes 1572868
  3.0 27.1 %copy-start.7 = (bf16[2,512,256]{2,1,0:T(8,128)(2,1)}, bf16[2,512,256]{2,1,0:T(8,128)(2,1)S(1)}, u32[]{:S(2)}) copy-start(bf16[2,512,256]{2,1,0:T(8,128)(2,1)S(1)} %get-tuple-element.18.rest_0_) | copy-start | bytes 1572868
  3.0 14.4 %collective-permute-start.4 = (bf16[2,512,256]{2,1,0:T(8,128)(2,1)S(1)}, bf16[2,512,256]{2,1,0:T(8,128)(2,1)S(1)}, u32[]{:S(2)}, u32[]{:S(2)}) collective-permute-start(bf16[2,512,256]{2,1,0:T(8,128)(2,1)S(1)} %get-tuple-element.19.rest_0_), channel_id=1, source_target_pairs={{4,0},{5,1},{6,2},{7,3},{0,4},{1,5},{2,6},{3,7},{12,8},{13,9},{14,... | collective-permute-start | bytes 1572872 | tf_op jit(solution)/shard_map/ppermute | solution.py:120
  4.2 15.9 %collective-permute-start = (bf16[2,512,256]{2,1,0:T(8,128)(2,1)S(1)}, bf16[2,512,256]{2,1,0:T(8,128)(2,1)S(1)}, u32[]{:S(2)}, u32[]{:S(2)}) collective-permute-start(bf16[2,512,256]{2,1,0:T(8,128)(2,1)S(1)} %get-tuple-element.17.rest_8_.rest_11_.rest_13_), channel_id=1, source_target_pairs={{3,0},{0,1},{1,2},{2,3},{7,4},{4,5},{5,6},{6,7},{9,8},{10,9},{11,1... | collective-permute-start | bytes 1572872 | tf_op jit(solution)/shard_map/ppermute | solution.py:120
  4.4 24.3 %collective-permute-start.3 = (bf16[2,512,256]{2,1,0:T(8,128)(2,1)S(1)}, bf16[2,512,256]{2,1,0:T(8,128)(2,1)S(1)}, u32[]{:S(2)}, u32[]{:S(2)}) collective-permute-start(bf16[2,512,256]{2,1,0:T(8,128)(2,1)S(1)} %get-tuple-element.18.rest_0_), channel_id=1, source_target_pairs={{4,0},{5,1},{6,2},{7,3},{0,4},{1,5},{2,6},{3,7},{12,8},{13,9},{14,... | collective-permute-start | bytes 1572872 | tf_op jit(solution)/shard_map/ppermute | solution.py:120
  17.4 12.7 %copy-start.2 = (bf16[2,512,256]{2,1,0:T(8,128)(2,1)}, bf16[2,512,256]{2,1,0:T(8,128)(2,1)S(1)}, u32[]{:S(2)}) copy-start(bf16[2,512,256]{2,1,0:T(8,128)(2,1)S(1)} %collective-permute-done.4.rest_12_.rest_15_) | copy-start | bytes 1572868
  17.4 12.0 %collective-permute-start.5 = (bf16[2,512,256]{2,1,0:T(8,128)(2,1)S(1)}, bf16[2,512,256]{2,1,0:T(8,128)(2,1)S(1)}, u32[]{:S(2)}, u32[]{:S(2)}) collective-permute-start(bf16[2,512,256]{2,1,0:T(8,128)(2,1)S(1)} %collective-permute-done.4.rest_12_.rest_15_), channel_id=1, source_target_pairs={{3,0},{0,1},{1,2},{2,3},{7,4},{4,5},{5,6},{6,7},{9,8},{10,9},{11,1... | collective-permute-start | bytes 1572872 | tf_op jit(solution)/shard_map/ppermute | solution.py:120
  17.5 14.1 %collective-permute-start.2 = (bf16[2,512,256]{2,1,0:T(8,128)(2,1)S(1)}, bf16[2,512,256]{2,1,0:T(8,128)(2,1)S(1)}, u32[]{:S(2)}, u32[]{:S(2)}) collective-permute-start(bf16[2,512,256]{2,1,0:T(8,128)(2,1)S(1)} %get-tuple-element.16.rest_0_.rest_3_.rest_1_), channel_id=1, source_target_pairs={{1,0},{2,1},{3,2},{0,3},{5,4},{6,5},{7,6},{4,7},{11,8},{8,9},{9,10... | collective-permute-start | bytes 1572872 | tf_op jit(solution)/shard_map/ppermute | solution.py:120
  20.1 20.7 %collective-permute-start.1 = (bf16[2,512,256]{2,1,0:T(8,128)(2,1)S(1)}, bf16[2,512,256]{2,1,0:T(8,128)(2,1)S(1)}, u32[]{:S(2)}, u32[]{:S(2)}) collective-permute-start(bf16[2,512,256]{2,1,0:T(8,128)(2,1)S(1)} %collective-permute-done.rest_1_.rest_9_.rest_12_), channel_id=1, source_target_pairs={{3,0},{0,1},{1,2},{2,3},{7,4},{4,5},{5,6},{6,7},{9,8},{10,9},{11,1... | collective-permute-start | bytes 1572872 | tf_op jit(solution)/shard_map/ppermute | solution.py:120
  28.7 14.3 %collective-permute-start.7 = (bf16[2,512,256]{2,1,0:T(8,128)(2,1)S(1)}, bf16[2,512,256]{2,1,0:T(8,128)(2,1)}, u32[]{:S(2)}, u32[]{:S(2)}) collective-permute-start(bf16[2,512,256]{2,1,0:T(8,128)(2,1)S(1)} %collective-permute-done.3.rest_4_.rest_7_.rest_5_), channel_id=1, source_target_pairs={{1,0},{2,1},{3,2},{0,3},{5,4},{6,5},{7,6},{4,7},{11,8},{8,9},{9,10... | collective-permute-start | bytes 1572872 | tf_op jit(solution)/shard_map/ppermute | solution.py:120
  29.4 19.8 %collective-permute-start.6 = (bf16[2,512,256]{2,1,0:T(8,128)(2,1)S(1)}, bf16[2,512,256]{2,1,0:T(8,128)(2,1)}, u32[]{:S(2)}, u32[]{:S(2)}) collective-permute-start(bf16[2,512,256]{2,1,0:T(8,128)(2,1)S(1)} %collective-permute-done.5.rest_5_.rest_13_.rest_16_.rest_11_), channel_id=1, source_target_pairs={{3,0},{0,1},{1,2},{2,3},{7,4},{4,5},{5,6},{6,7},{9,8},{10,9},{11,1... | collective-permute-start | bytes 1572872 | tf_op jit(solution)/shard_map/ppermute | solution.py:120
  30.1 30.0 %collective-permute-start.21 = (bf16[2,512,256]{2,1,0:T(8,128)(2,1)S(1)}, bf16[2,512,256]{2,1,0:T(8,128)(2,1)}, u32[]{:S(2)}, u32[]{:S(2)}) collective-permute-start(bf16[2,512,256]{2,1,0:T(8,128)(2,1)S(1)} %get-tuple-element.16.rest_0_.rest_3_.rest_1_), channel_id=1, source_target_pairs={{3,0},{0,1},{1,2},{2,3},{7,4},{4,5},{5,6},{6,7},{9,8},{10,9},{11,1... | collective-permute-start | bytes 1572872 | tf_op jit(solution)/shard_map/ppermute | solution.py:120
  30.3 23.2 %copy-start.1 = (bf16[2,512,256]{2,1,0:T(8,128)(2,1)S(1)}, bf16[2,512,256]{2,1,0:T(8,128)(2,1)}, u32[]{:S(2)}) copy-start(bf16[2,512,256]{2,1,0:T(8,128)(2,1)} %copy-done) | copy-start | bytes 1572868
  30.3 29.8 %copy-start.6 = (bf16[2,512,256]{2,1,0:T(8,128)(2,1)S(1)}, bf16[2,512,256]{2,1,0:T(8,128)(2,1)}, u32[]{:S(2)}) copy-start(bf16[2,512,256]{2,1,0:T(8,128)(2,1)} %copy-done.5) | copy-start | bytes 1572868
  30.3 42.2 %copy-start.8 = (bf16[2,512,256]{2,1,0:T(8,128)(2,1)S(1)}, bf16[2,512,256]{2,1,0:T(8,128)(2,1)}, u32[]{:S(2)}) copy-start(bf16[2,512,256]{2,1,0:T(8,128)(2,1)} %copy-done.7) | copy-start | bytes 1572868
  30.4 58.6 %copy-start.3 = (bf16[2,512,256]{2,1,0:T(8,128)(2,1)S(1)}, bf16[2,512,256]{2,1,0:T(8,128)(2,1)}, u32[]{:S(2)}) copy-start(bf16[2,512,256]{2,1,0:T(8,128)(2,1)} %copy-done.2) | copy-start | bytes 1572868
  51.0 111.5 %copy-start.9 = (s32[1,15]{1,0:T(1,128)S(1)}, s32[1,15]{1,0:T(1,128)}, u32[]{:S(2)}) copy-start(s32[1,15]{1,0:T(1,128)} %neighbours.11) | copy-start | bytes 184
  51.0 63.2 %collective-permute-start.37 = (bf16[512,2048]{1,0:T(8,128)(2,1)S(1)}, bf16[512,2048]{1,0:T(8,128)(2,1)S(1)}, u32[]{:S(2)}, u32[]{:S(2)}) collective-permute-start(bf16[512,2048]{1,0:T(8,128)(2,1)S(1)} %weigh.1.weights), channel_id=1, source_target_pairs={{12,16},{13,17},{14,18},{15,19},{16,12},{17,13},{18,14},{19,15},{2... | collective-permute-start | bytes 6291464 | tf_op jit(solution)/shard_map/ppermute | solution.py:120
  53.6 13.0 %collective-permute-start.22 = (bf16[2,512,256]{2,1,0:T(8,128)(2,1)S(1)}, bf16[2,512,256]{2,1,0:T(8,128)(2,1)S(1)}, u32[]{:S(2)}, u32[]{:S(2)}) collective-permute-start(bf16[2,512,256]{2,1,0:T(8,128)(2,1)S(1)} %copy-done.1), channel_id=1, source_target_pairs={{1,0},{2,1},{3,2},{0,3},{5,4},{6,5},{7,6},{4,7},{11,8},{8,9},{9,10... | collective-permute-start | bytes 1572872 | tf_op jit(solution)/shard_map/ppermute | solution.py:120
  57.1 15.4 %collective-permute-start.12 = (bf16[2,512,256]{2,1,0:T(8,128)(2,1)S(1)}, bf16[2,512,256]{2,1,0:T(8,128)(2,1)S(1)}, u32[]{:S(2)}, u32[]{:S(2)}) collective-permute-start(bf16[2,512,256]{2,1,0:T(8,128)(2,1)S(1)} %get-tuple-element.16.rest_0_.rest_3_.rest_1_), channel_id=1, source_target_pairs={{4,0},{5,1},{6,2},{7,3},{0,4},{1,5},{2,6},{3,7},{12,8},{13,9},{14,... | collective-permute-start | bytes 1572872 | tf_op jit(solution)/shard_map/ppermute | solution.py:120
  57.1 22.4 %collective-permute-start.13 = (bf16[2,512,256]{2,1,0:T(8,128)(2,1)S(1)}, bf16[2,512,256]{2,1,0:T(8,128)(2,1)S(1)}, u32[]{:S(2)}, u32[]{:S(2)}) collective-permute-start(bf16[2,512,256]{2,1,0:T(8,128)(2,1)S(1)} %copy-done.1), channel_id=1, source_target_pairs={{4,0},{5,1},{6,2},{7,3},{0,4},{1,5},{2,6},{3,7},{12,8},{13,9},{14,... | collective-permute-start | bytes 1572872 | tf_op jit(solution)/shard_map/ppermute | solution.py:120
  60.1 20.5 %collective-permute-start.9 = (bf16[2,512,256]{2,1,0:T(8,128)(2,1)S(1)}, bf16[2,512,256]{2,1,0:T(8,128)(2,1)S(1)}, u32[]{:S(2)}, u32[]{:S(2)}) collective-permute-start(bf16[2,512,256]{2,1,0:T(8,128)(2,1)S(1)} %copy-done.6), channel_id=1, source_target_pairs={{3,0},{0,1},{1,2},{2,3},{7,4},{4,5},{5,6},{6,7},{9,8},{10,9},{11,1... | collective-permute-start | bytes 1572872 | tf_op jit(solution)/shard_map/ppermute | solution.py:120
  66.5 69.4 %collective-permute-start.32 = (bf16[512,2048]{1,0:T(8,128)(2,1)S(1)}, bf16[512,2048]{1,0:T(8,128)(2,1)S(1)}, u32[]{:S(2)}, u32[]{:S(2)}) collective-permute-start(bf16[512,2048]{1,0:T(8,128)(2,1)S(1)} %weigh.1.weights), channel_id=1, source_target_pairs={{24,56},{25,57},{26,58},{27,59},{28,60},{29,61},{30,62},{31,63},{3... | collective-permute-start | bytes 6291464 | tf_op jit(solution)/shard_map/ppermute | solution.py:120
  72.6 8.2 %collective-permute-start.11 = (bf16[2,512,256]{2,1,0:T(8,128)(2,1)S(1)}, bf16[2,512,256]{2,1,0:T(8,128)(2,1)S(1)}, u32[]{:S(2)}, u32[]{:S(2)}) collective-permute-start(bf16[2,512,256]{2,1,0:T(8,128)(2,1)S(1)} %copy-done.8), channel_id=1, source_target_pairs={{1,0},{2,1},{3,2},{0,3},{5,4},{6,5},{7,6},{4,7},{11,8},{8,9},{9,10... | collective-permute-start | bytes 1572872 | tf_op jit(solution)/shard_map/ppermute | solution.py:120
  79.5 9.4 %collective-permute-start.17 = (bf16[2,512,256]{2,1,0:T(8,128)(2,1)S(1)}, bf16[2,512,256]{2,1,0:T(8,128)(2,1)S(1)}, u32[]{:S(2)}, u32[]{:S(2)}) collective-permute-start(bf16[2,512,256]{2,1,0:T(8,128)(2,1)S(1)} %copy-done.8), channel_id=1, source_target_pairs={{3,0},{0,1},{1,2},{2,3},{7,4},{4,5},{5,6},{6,7},{9,8},{10,9},{11,1... | collective-permute-start | bytes 1572872 | tf_op jit(solution)/shard_map/ppermute | solution.py:120
  80.6 15.5 %collective-permute-start.23 = (bf16[2,512,256]{2,1,0:T(8,128)(2,1)S(1)}, bf16[2,512,256]{2,1,0:T(8,128)(2,1)S(1)}, u32[]{:S(2)}, u32[]{:S(2)}) collective-permute-start(bf16[2,512,256]{2,1,0:T(8,128)(2,1)S(1)} %collective-permute-done.3.rest_4_.rest_7_.rest_5_), channel_id=1, source_target_pairs={{3,0},{0,1},{1,2},{2,3},{7,4},{4,5},{5,6},{6,7},{9,8},{10,9},{11,1... | collective-permute-start | bytes 1572872 | tf_op jit(solution)/shard_map/ppermute | solution.py:120
  80.8 25.0 %collective-permute-start.25 = (bf16[2,512,256]{2,1,0:T(8,128)(2,1)}, bf16[2,512,256]{2,1,0:T(8,128)(2,1)S(1)}, u32[]{:S(2)}, u32[]{:S(2)}) collective-permute-start(bf16[2,512,256]{2,1,0:T(8,128)(2,1)} %collective-permute-done.21.rest_1_.rest_4_.rest_2_), channel_id=1, source_target_pairs={{3,0},{0,1},{1,2},{2,3},{7,4},{4,5},{5,6},{6,7},{9,8},{10,9},{11,1... | collective-permute-start | bytes 1572872 | tf_op jit(solution)/shard_map/ppermute | solution.py:120
  88.9 18.6 %collective-permute-start.24 = (bf16[2,512,256]{2,1,0:T(8,128)(2,1)S(1)}, bf16[2,512,256]{2,1,0:T(8,128)(2,1)S(1)}, u32[]{:S(2)}, u32[]{:S(2)}) collective-permute-start(bf16[2,512,256]{2,1,0:T(8,128)(2,1)S(1)} %copy-done.3), channel_id=1, source_target_pairs={{1,0},{2,1},{3,2},{0,3},{5,4},{6,5},{7,6},{4,7},{11,8},{8,9},{9,10... | collective-permute-start | bytes 1572872 | tf_op jit(solution)/shard_map/ppermute | solution.py:120
  96.1 16.9 %collective-permute-start.26 = (bf16[2,512,256]{2,1,0:T(8,128)(2,1)S(1)}, bf16[2,512,256]{2,1,0:T(8,128)(2,1)S(1)}, u32[]{:S(2)}, u32[]{:S(2)}) collective-permute-start(bf16[2,512,256]{2,1,0:T(8,128)(2,1)S(1)} %collective-permute-done.23.rest_5_.rest_8_.rest_6_), channel_id=1, source_target_pairs={{3,0},{0,1},{1,2},{2,3},{7,4},{4,5},{5,6},{6,7},{9,8},{10,9},{11,1... | collective-permute-start | bytes 1572872 | tf_op jit(solution)/shard_map/ppermute | solution.py:120
  105.8 16.2 %collective-permute-start.18 = (bf16[2,512,256]{2,1,0:T(8,128)(2,1)S(1)}, bf16[2,512,256]{2,1,0:T(8,128)(2,1)S(1)}, u32[]{:S(2)}, u32[]{:S(2)}) collective-permute-start(bf16[2,512,256]{2,1,0:T(8,128)(2,1)S(1)} %copy-done.6), channel_id=1, source_target_pairs={{1,0},{2,1},{3,2},{0,3},{5,4},{6,5},{7,6},{4,7},{11,8},{8,9},{9,10... | collective-permute-start | bytes 1572872 | tf_op jit(solution)/shard_map/ppermute | solution.py:120
  107.5 16.7 %collective-permute-start.19 = (bf16[2,512,256]{2,1,0:T(8,128)(2,1)S(1)}, bf16[2,512,256]{2,1,0:T(8,128)(2,1)S(1)}, u32[]{:S(2)}, u32[]{:S(2)}) collective-permute-start(bf16[2,512,256]{2,1,0:T(8,128)(2,1)S(1)} %collective-permute-done.12.rest_4_), channel_id=1, source_target_pairs={{3,0},{0,1},{1,2},{2,3},{7,4},{4,5},{5,6},{6,7},{9,8},{10,9},{11,1... | collective-permute-start | bytes 1572872 | tf_op jit(solution)/shard_map/ppermute | solution.py:120
  113.0 18.0 %collective-permute-start.16 = (bf16[2,512,256]{2,1,0:T(8,128)(2,1)S(1)}, bf16[2,512,256]{2,1,0:T(8,128)(2,1)S(1)}, u32[]{:S(2)}, u32[]{:S(2)}) collective-permute-start(bf16[2,512,256]{2,1,0:T(8,128)(2,1)S(1)} %collective-permute-done.12.rest_4_), channel_id=1, source_target_pairs={{1,0},{2,1},{3,2},{0,3},{5,4},{6,5},{7,6},{4,7},{11,8},{8,9},{9,10... | collective-permute-start | bytes 1572872 | tf_op jit(solution)/shard_map/ppermute | solution.py:120
  114.2 19.7 %collective-permute-start.14 = (bf16[2,512,256]{2,1,0:T(8,128)(2,1)S(1)}, bf16[2,512,256]{2,1,0:T(8,128)(2,1)S(1)}, u32[]{:S(2)}, u32[]{:S(2)}) collective-permute-start(bf16[2,512,256]{2,1,0:T(8,128)(2,1)S(1)} %collective-permute-done.13.rest_4_), channel_id=1, source_target_pairs={{3,0},{0,1},{1,2},{2,3},{7,4},{4,5},{5,6},{6,7},{9,8},{10,9},{11,1... | collective-permute-start | bytes 1572872 | tf_op jit(solution)/shard_map/ppermute | solution.py:120
  122.0 52.1 %collective-permute-start.31 = (bf16[512,2048]{1,0:T(8,128)(2,1)S(1)}, bf16[512,2048]{1,0:T(8,128)(2,1)S(1)}, u32[]{:S(2)}, u32[]{:S(2)}) collective-permute-start(bf16[512,2048]{1,0:T(8,128)(2,1)S(1)} %weigh.1.weights), channel_id=1, source_target_pairs={{8,16},{9,17},{10,18},{11,19},{12,20},{13,21},{14,22},{15,23},{16,... | collective-permute-start | bytes 6291464 | tf_op jit(solution)/shard_map/ppermute | solution.py:120
  124.2 49.9 %collective-permute-start.8 = (bf16[512,2048]{1,0:T(8,128)(2,1)S(1)}, bf16[512,2048]{1,0:T(8,128)(2,1)S(1)}, u32[]{:S(2)}, u32[]{:S(2)}) collective-permute-start(bf16[512,2048]{1,0:T(8,128)(2,1)S(1)} %weigh.1.weights), channel_id=1, source_target_pairs={{0,8},{1,9},{2,10},{3,11},{4,12},{5,13},{6,14},{7,15},{8,0},{9,1},... | collective-permute-start | bytes 6291464 | tf_op jit(solution)/shard_map/ppermute | solution.py:120
  131.0 44.2 %collective-permute-start.39 = (bf16[4,512,512]{2,1,0:T(8,128)(2,1)S(1)}, bf16[4,512,512]{2,1,0:T(8,128)(2,1)S(1)}, u32[]{:S(2)}, u32[]{:S(2)}) collective-permute-start(bf16[4,512,512]{2,1,0:T(8,128)(2,1)S(1)} %ask_products.3), channel_id=1, source_target_pairs={{28,60},{29,61},{30,62},{31,63},{32,0},{33,1},{34,2},{35,3},{60,92... | collective-permute-start | bytes 6291464 | tf_op jit(solution)/shard_map/ppermute | solution.py:120
  133.9 8.3 %collective-permute-start.20 = (bf16[2,512,256]{2,1,0:T(8,128)(2,1)S(1)}, bf16[2,512,256]{2,1,0:T(8,128)(2,1)S(1)}, u32[]{:S(2)}, u32[]{:S(2)}) collective-permute-start(bf16[2,512,256]{2,1,0:T(8,128)(2,1)S(1)} %collective-permute-done.13.rest_4_), channel_id=1, source_target_pairs={{1,0},{2,1},{3,2},{0,3},{5,4},{6,5},{7,6},{4,7},{11,8},{8,9},{9,10... | collective-permute-start | bytes 1572872 | tf_op jit(solution)/shard_map/ppermute | solution.py:120
  135.9 57.8 %collective-permute-start.33 = (bf16[512,2048]{1,0:T(8,128)(2,1)S(1)}, bf16[512,2048]{1,0:T(8,128)(2,1)S(1)}, u32[]{:S(2)}, u32[]{:S(2)}) collective-permute-start(bf16[512,2048]{1,0:T(8,128)(2,1)S(1)} %collective-permute-done.32), channel_id=1, source_target_pairs={{56,32},{57,33},{58,34},{59,35},{60,36},{61,37},{62,38},{63,39},{0... | collective-permute-start | bytes 6291464 | tf_op jit(solution)/shard_map/ppermute | solution.py:120
  142.2 9.5 %collective-permute-start.10 = (bf16[2,512,256]{2,1,0:T(8,128)(2,1)S(1)}, bf16[2,512,256]{2,1,0:T(8,128)(2,1)S(1)}, u32[]{:S(2)}, u32[]{:S(2)}) collective-permute-start(bf16[2,512,256]{2,1,0:T(8,128)(2,1)S(1)} %collective-permute-done.9.rest_1_), channel_id=1, source_target_pairs={{3,0},{0,1},{1,2},{2,3},{7,4},{4,5},{5,6},{6,7},{9,8},{10,9},{11,1... | collective-permute-start | bytes 1572872 | tf_op jit(solution)/shard_map/ppermute | solution.py:120
  151.7 9.2 %collective-permute-start.15 = (bf16[2,512,256]{2,1,0:T(8,128)(2,1)S(1)}, bf16[2,512,256]{2,1,0:T(8,128)(2,1)S(1)}, u32[]{:S(2)}, u32[]{:S(2)}) collective-permute-start(bf16[2,512,256]{2,1,0:T(8,128)(2,1)S(1)} %collective-permute-done.14.rest_5_), channel_id=1, source_target_pairs={{3,0},{0,1},{1,2},{2,3},{7,4},{4,5},{5,6},{6,7},{9,8},{10,9},{11,1... | collective-permute-start | bytes 1572872 | tf_op jit(solution)/shard_map/ppermute | solution.py:120
  161.0 52.1 %collective-permute-start.38 = (bf16[4,512,512]{2,1,0:T(8,128)(2,1)S(1)}, bf16[4,512,512]{2,1,0:T(8,128)(2,1)S(1)}, u32[]{:S(2)}, u32[]{:S(2)}) collective-permute-start(bf16[4,512,512]{2,1,0:T(8,128)(2,1)S(1)} %ask_products.3), channel_id=1, source_target_pairs={{12,16},{13,17},{14,18},{15,19},{16,12},{17,13},{18,14},{19,15},{4... | collective-permute-start | bytes 6291464 | tf_op jit(solution)/shard_map/ppermute | solution.py:120
  174.0 27.8 %collective-permute-start.29 = (bf16[2,512,256]{2,1,0:T(8,128)(2,1)S(1)}, bf16[2,512,256]{2,1,0:T(8,128)(2,1)S(1)}, u32[]{:S(2)}, u32[]{:S(2)}) collective-permute-start(bf16[2,512,256]{2,1,0:T(8,128)(2,1)S(1)} %collective-permute-done.19.rest_10_), channel_id=1, source_target_pairs={{3,0},{0,1},{1,2},{2,3},{7,4},{4,5},{5,6},{6,7},{9,8},{10,9},{11,1... | collective-permute-start | bytes 1572872 | tf_op jit(solution)/shard_map/ppermute | solution.py:120
  174.1 27.7 %collective-permute-start.28 = (bf16[2,512,256]{2,1,0:T(8,128)(2,1)S(1)}, bf16[2,512,256]{2,1,0:T(8,128)(2,1)S(1)}, u32[]{:S(2)}, u32[]{:S(2)}) collective-permute-start(bf16[2,512,256]{2,1,0:T(8,128)(2,1)S(1)} %collective-permute-done.26.rest_14_.rest_17_.rest_16_), channel_id=1, source_target_pairs={{4,0},{5,1},{6,2},{7,3},{0,4},{1,5},{2,6},{3,7},{12,8},{13,9},{14,... | collective-permute-start | bytes 1572872 | tf_op jit(solution)/shard_map/ppermute | solution.py:120
  175.1 55.0 %collective-permute-start.40 = (bf16[4,512,512]{2,1,0:T(8,128)(2,1)S(1)}, bf16[4,512,512]{2,1,0:T(8,128)(2,1)S(1)}, u32[]{:S(2)}, u32[]{:S(2)}) collective-permute-start(bf16[4,512,512]{2,1,0:T(8,128)(2,1)S(1)} %collective-permute-done.39), channel_id=1, source_target_pairs={{60,32},{61,33},{62,34},{63,35},{0,28},{1,29},{2,30},{3,31},{92,64... | collective-permute-start | bytes 6291464 | tf_op jit(solution)/shard_map/ppermute | solution.py:120
  199.8 15.2 %collective-permute-start.34 = (bf16[512,512]{1,0:T(8,128)(2,1)S(1)}, bf16[512,512]{1,0:T(8,128)(2,1)S(1)}, u32[]{:S(2)}, u32[]{:S(2)}) collective-permute-start(bf16[512,512]{1,0:T(8,128)(2,1)S(1)} %get-tuple-element.23), channel_id=1, source_target_pairs={{0,8},{4,12},{8,16},{9,17},{10,18},{11,3},{12,20},{13,21},{14,22},... | collective-permute-start | bytes 1572872 | tf_op jit(solution)/shard_map/ppermute | solution.py:120
  210.4 22.9 %collective-permute-start.30 = (bf16[2,512,512]{2,1,0:T(8,128)(2,1)S(1)}, bf16[2,512,512]{2,1,0:T(8,128)(2,1)S(1)}, u32[]{:S(2)}, u32[]{:S(2)}) collective-permute-start(bf16[2,512,512]{2,1,0:T(8,128)(2,1)S(1)} %get-tuple-element.22), channel_id=1, source_target_pairs={{0,8},{1,9},{2,10},{3,11},{12,4},{13,5},{14,6},{15,7},{16,24},{17,... | collective-permute-start | bytes 3145736 | tf_op jit(solution)/shard_map/ppermute | solution.py:120
  211.7 21.6 %collective-permute-start.27 = (bf16[2,512,512]{2,1,0:T(8,128)(2,1)S(1)}, bf16[2,512,512]{2,1,0:T(8,128)(2,1)S(1)}, u32[]{:S(2)}, u32[]{:S(2)}) collective-permute-start(bf16[2,512,512]{2,1,0:T(8,128)(2,1)S(1)} %get-tuple-element.20), channel_id=1, source_target_pairs={{0,8},{1,9},{2,10},{3,11},{12,4},{13,5},{14,6},{15,7},{16,24},{17,... | collective-permute-start | bytes 3145736 | tf_op jit(solution)/shard_map/ppermute | solution.py:120
  213.1 11.4 %collective-permute-start.35 = (bf16[512,512]{1,0:T(8,128)(2,1)S(1)}, bf16[512,512]{1,0:T(8,128)(2,1)S(1)}, u32[]{:S(2)}, u32[]{:S(2)}) collective-permute-start(bf16[512,512]{1,0:T(8,128)(2,1)S(1)} %get-tuple-element.24), channel_id=1, source_target_pairs={{0,8},{1,9},{2,10},{4,12},{5,13},{6,14},{8,16},{9,1},{10,2},{11,3}... | collective-permute-start | bytes 1572872 | tf_op jit(solution)/shard_map/ppermute | solution.py:120
  215.0 15.1 %collective-permute-start.36 = (bf16[512,512]{1,0:T(8,128)(2,1)S(1)}, bf16[512,512]{1,0:T(8,128)(2,1)S(1)}, u32[]{:S(2)}, u32[]{:S(2)}) collective-permute-start(bf16[512,512]{1,0:T(8,128)(2,1)S(1)} %get-tuple-element.25), channel_id=1, source_target_pairs={{0,8},{1,9},{4,12},{5,13},{8,16},{9,17},{10,2},{11,3},{12,20},{13,... | collective-permute-start | bytes 1572872 | tf_op jit(solution)/shard_map/ppermute | solution.py:120
